TPU v7x, 128 devices: a whole 4x4x4 slice. The times are simulated.
128 devices in a mesh: row: 4 (over y), col: 4 (over z), depth: 8 (over x, core).
Axes of the slice: x: 4, y: 4, z: 4, core: 2. Of those that a mesh axis runs over, the one named last changes fastest.
Arguments:
- diag_block: float32 [512, 512], P(('row', 'col', 'depth')), as said below
- panel_rows: float32 [32256, 512], P(('row', 'col', 'depth')), may hold values from -2 to 2
- trailing: float32 [32256, 1024], P(('row', 'depth'), 'col'), may hold values from -6 to 6
Outputs:
- diag_factor: float32 [512, 512], P(('row', 'col', 'depth'))
- panel_factor: float32 [32256, 512], P(('row', 'col', 'depth'))
- updated: float32 [32256, 1024], P(('row', 'depth'), 'col')
Inputs may be any that keep to these rules, and one draw needn't show every extreme that they name: `diag_block`: symmetric positive definite.
All inputs are finite; a program needn't handle non-finite values.
Results may differ from a plain program's by a relative error of at most 0.000062.
Values sent between devices are 32-bit elements; how exact they have to be, the bound alone decides.
A program may use at most 64 MiB of HBM per device.

v0:
```python
import jax
import jax.numpy as jnp
from jax import lax
from jax.experimental import pallas as pl
from jax.experimental.pallas import tpu as pltpu
from jax.sharding import PartitionSpec as P

ALL = ("row", "col", "depth")
F32 = jnp.float32
NT = (((1,), (1,)), ((), ()))
BLOCK = 128
MESH = pl.DeviceIdType.MESH


def at(i):
    return slice(BLOCK * i, BLOCK * (i + 1))


def split(x):
    hi = x.astype(jnp.bfloat16)
    return hi, (x - hi.astype(F32)).astype(jnp.bfloat16)


def dot(a, b):
    def one(x, y):
        return lax.dot_general(x, y, NT, preferred_element_type=F32)

    return one(a[0], b[0]) + (one(a[0], b[1]) + one(a[1], b[0]))


def sub(v, k):
    return jnp.broadcast_to(v[k : k + 1, :], (8, 128))


class Block:
    def __init__(self, rows):
        self.ri = lax.broadcasted_iota(jnp.int32, (8, 128), 0)
        self.li = lax.broadcasted_iota(jnp.int32, (8, 128), 1)
        self.rows = rows
        self.unit = jnp.stack([jnp.where(self.li == self.ri + 8 * v, 1.0, 0.0).astype(F32) for v in range(16)])
        self.upper, self.inverse = [], []

    def advance(self, panels):
        ri, li = self.ri, self.li
        for p in panels:
            rows, unit = self.rows, self.unit
            cols = [jnp.broadcast_to(rows[:, :, 8 * p + j : 8 * p + j + 1], rows.shape) for j in range(8)]
            r = [sub(rows[0], k) for k in range(8)]
            s = [sub(unit[0], k) for k in range(8)]
            for k in range(8):
                inv = lax.rsqrt(sub(cols[k][0], k))
                cols[k] = cols[k] * inv
                r[k] = r[k] * inv
                s[k] = s[k] * inv
                for j in range(k + 1, 8):
                    m = sub(cols[k][0], j)
                    cols[j] = cols[j] - cols[k] * m
                    r[j] = r[j] - m * r[k]
                    s[j] = s[j] - m * s[k]
            u, t = r[0], s[0]
            for k in range(1, 8):
                u = jnp.where(ri == k, r[k], u)
                t = jnp.where(ri == k, s[k], t)
            self.upper.append(jnp.where(li >= ri + 8 * p, u, 0.0))
            self.inverse.append(t)
            if p < 15:
                rows, unit = rows[1:], unit[1:]
                for k in range(8):
                    rows = rows - cols[k][1:] * r[k]
                    unit = unit - cols[k][1:] * s[k]
                self.rows, self.unit = rows, unit


class Factor:
    def __init__(self, a, l, schur):
        self.a, self.l, self.schur = a, l, schur
        self.lows, self.invs = {}, {}

    def block(self, k, between=lambda: None):
        src = self.a if k == 0 else self.schur
        b = Block(jnp.stack([src[BLOCK * k + 8 * v : BLOCK * k + 8 * v + 8, at(k)] for v in range(16)]))
        b.advance(range(8))
        between()
        b.advance(range(8, 16))
        self.invs[k] = split(jnp.concatenate(b.inverse, 0))
        self.l[at(k), at(k)] = jnp.concatenate(b.upper, 0).T
        for j in range(k + 1, 4):
            self.l[at(k), at(j)] = jnp.zeros((BLOCK, BLOCK), F32)

    def rest(self, k):
        src = self.a if k == 0 else self.schur
        for i in range(k + 1, 4):
            low = dot(split(src[at(i), at(k)]), self.invs[k])
            self.l[at(i), at(k)] = low
            self.lows[i, k] = split(low)
        for j in range(k + 1, 4):
            for i in range(j, 4):
                self.schur[at(i), at(j)] = src[at(i), at(j)] - dot(self.lows[i, k], self.lows[j, k])

    def solve_block(self, x, k, done):
        for m in range(k):
            x = x - dot(done[m][1], self.lows[k, m])
        value = dot(split(x), self.invs[k])
        done.append((value, split(value)))


def remote(src, dst, send, recv, **device):
    return pltpu.make_async_remote_copy(
        src_ref=src, dst_ref=dst, send_sem=send, recv_sem=recv, device_id=device, device_id_type=MESH
    )


class Exchange:
    def __init__(self, diag, panel, dbuf, relay, rows, win, wsrc, pw, q, sems):
        self.diag, self.panel, self.dbuf, self.relay, self.rows = diag, panel, dbuf, relay, rows
        self.win, self.wsrc, self.pw, self.q = win, wsrc, pw, q
        (self.loc, self.ds, self.dr, self.cs, self.cr, self.rs, self.rr, self.zs, self.zr, self.xs, self.xr,
         self.w1s, self.w1r, self.w2s, self.w2r, self.w3s, self.w3r, self.w4s, self.w4r, self.w5s, self.w5r) = sems
        self.r, self.c, self.s = (lax.axis_index(a) for a in ALL)
        self.corner = jnp.logical_and(self.r == 0, self.c == 0)

    def enter(self):
        r, c, s = self.r, self.c, self.s
        self.own_diag = pltpu.make_async_copy(self.diag, self.dbuf.at[r, c, s], self.loc.at[0])
        self.own_panel = pltpu.make_async_copy(self.panel, self.relay.at[c], self.loc.at[1])
        self.own_diag.start()
        self.own_panel.start()
        barrier = pltpu.get_barrier_semaphore()
        for axis, me, n in (("depth", s, 8), ("col", c, 4), ("row", r, 4)):
            for t in range(1, n):
                pl.semaphore_signal(barrier, inc=1, device_id={axis: (me + t) % n}, device_id_type=MESH)
        pl.semaphore_wait(barrier, 13)
        self.own_diag.wait()

    def diag_col(self, t, c):
        ref = self.dbuf.at[self.r, c, self.s]
        return remote(ref, ref, self.cs.at[t], self.cr.at[t], col=(self.c + t) % 4)

    def diag_col_send(self):
        for t in range(1, 4):
            self.diag_col(t, self.c).start()

    def diag_col_wait(self):
        for t in range(1, 4):
            self.diag_col(t, (self.c - t) % 4).wait_recv()

    def diag_depth(self, t, s, i):
        ref = self.dbuf.at[i, :, s, :, 0 : 128 * (i + 1)]
        return remote(ref, ref, self.ds.at[t], self.dr.at[t], depth=(self.s + t) % 8)

    def by_row(self, act):
        for i in range(4):

            @pl.when(self.r == i)
            def _():
                act(i)

    def diag_depth_send(self):
        self.by_row(lambda i: [self.diag_depth(t, self.s, i).start() for t in range(1, 8)] and None)

    def diag_depth_wait(self):
        self.by_row(lambda i: [self.diag_depth(t, (self.s - t) % 8, i).wait_recv() for t in range(1, 8)] and None)

    def diag_row(self, t, i):
        ref = self.dbuf.at[i, :, :, :, 0 : 128 * (i + 1)]
        return remote(ref, ref, self.rs.at[t], self.rr.at[t], row=(self.r + t) % 4)

    def diag_row_send(self):
        self.by_row(lambda i: [self.diag_row(t, i).start() for t in range(1, 4)] and None)

    def diag_row_wait(self, src):
        self.by_row(lambda i: None if i == src else self.diag_row((i - src) % 4, src).wait_recv())

    def rows_col(self, t, slot, b):
        ref = self.relay.at[slot, :, at(b)]
        return remote(ref, ref, self.zs.at[t, b], self.zr.at[t, b], col=(self.c + t) % 4)

    def rows_col_send(self, b):
        for t in (1, 3, 2):
            self.rows_col(t, self.c, b).start()

    def rows_pass(self, b):
        for t in (1, 3, 2):
            slot = (self.c - t) % 4
            self.rows_col(t, slot, b).wait_recv()
            self.rows_depth_send(t, slot, b)

    def rows_depth(self, t, slot, b):
        target, j = 2 * slot + self.s // 4, self.s % 4
        return target, remote(
            self.relay.at[slot, :, at(b)], self.rows.at[j, :, at(b)], self.xs.at[t, b], self.xr.at[j, b], depth=target
        )

    def rows_depth_send(self, t, slot, b):
        target, copy = self.rows_depth(t, slot, b)

        @pl.when(target != self.s)
        def _():
            copy.start()

        @pl.when(target == self.s)
        def _():
            self.rows[self.s % 4, :, at(b)] = self.relay[slot, :, at(b)]

    def rows_wait(self, b):
        for j in range(4):
            source = 4 * (self.s % 2) + j
            ref = self.rows.at[j, :, at(b)]

            @pl.when(source != self.s)
            def _():
                remote(ref, ref, self.xs.at[0, b], self.xr.at[j, b], depth=source).wait_recv()

    def win_main(self, i, d):
        n = 8 if d < 7 else 7 - i
        return remote(
            self.wsrc.at[i + 8 * d : i + 8 * d + n], self.pw.at[i, 0:n], self.w1s.at[d], self.w1r.at[i], depth=d
        )

    def win_head(self, c):
        return remote(self.wsrc.at[0 : c + 1], self.pw.at[c, 7 - c : 8], self.w1s.at[8], self.w1r.at[4 + c], depth=7)

    def win_scatter(self, act):
        for i in range(5):

            @pl.when(jnp.logical_and(self.corner, self.s == i))
            def _():
                if i < 4:
                    for d in range(8):
                        if d != i:
                            act(self.win_main(i, d))
                if i > 0:
                    act(self.win_head(i - 1))

    def win_scatter_send(self):
        @pl.when(jnp.logical_and(self.corner, self.s < 5))
        def _():
            for u in range(63):
                self.wsrc[u] = self.relay[0, 4 * u : 4 * u + 4, :]

        for i in range(4):

            @pl.when(jnp.logical_and(self.corner, self.s == i))
            def _():
                self.pw[i] = self.wsrc[9 * i : 9 * i + 8]

        self.win_scatter(lambda copy: copy.start())

    def win_scatter_wait(self):
        for d in range(8):

            @pl.when(jnp.logical_and(self.corner, self.s == d))
            def _():
                for i in range(4):
                    if d != i:
                        self.win_main(i, d).wait_recv()
                    if d == 7:
                        self.win_head(i).wait_recv()

    def win_col(self, t):
        return remote(self.pw.at[t], self.q, self.w2s.at[t], self.w2r.at[0], col=t)

    def win_col_send(self):
        @pl.when(self.corner)
        def _():
            for t in range(1, 4):
                self.win_col(t).start()
            self.q[...] = self.pw[0]

    def win_col_wait(self):
        @pl.when(jnp.logical_and(self.r == 0, self.c != 0))
        def _():
            self.win_col(1).wait_recv()

    def win_row(self, t, row):
        return remote(
            self.q.at[2 * t : 2 * t + 2], self.win.at[self.s, row], self.w3s.at[t], self.w3r.at[0], row=t
        )

    def win_row_send(self):
        @pl.when(self.r == 0)
        def _():
            for t in range(1, 4):
                self.win_row(t, t).start()
            self.win[self.s, 0] = self.q[0:2]

    def win_row_wait(self):
        @pl.when(self.r != 0)
        def _():
            self.win_row(1, self.r).wait_recv()

    def win_depth(self, t, d):
        ref = self.win.at[d, self.r]
        return remote(ref, ref, self.w4s.at[t], self.w4r.at[t], depth=(self.s + t) % 8)

    def win_depth_send(self):
        for t in range(1, 8):
            self.win_depth(t, self.s).start()

    def win_depth_wait(self):
        for t in range(1, 8):
            self.win_depth(t, (self.s - t) % 8).wait_recv()

    def win_all(self, t, row):
        ref = self.win.at[:, row]
        return remote(ref, ref, self.w5s.at[t], self.w5r.at[t], row=(self.r + t) % 4)

    def win_all_send(self):
        for t in range(1, 4):
            self.win_all(t, self.r).start()

    def win_all_wait(self):
        for t in range(1, 4):
            self.win_all(t, (self.r - t) % 4).wait_recv()

    def leave(self):
        for t in range(1, 8):
            self.win_depth(t, self.s).wait_send()
        self.by_row(
            lambda i: [self.diag_depth(t, self.s, i).wait_send() for t in range(1, 8)]
            and [self.diag_row(t, i).wait_send() for t in range(1, 4)]
            and None
        )
        for t in range(1, 4):
            self.diag_col(t, self.c).wait_send()
            self.win_all(t, self.r).wait_send()
        for b in range(4):
            for t in range(4):
                if t:
                    self.rows_col(t, self.c, b).wait_send()
                target, copy = self.rows_depth(t, (self.c - t) % 4, b)

                @pl.when(target != self.s)
                def _():
                    copy.wait_send()

        self.win_scatter(lambda copy: copy.wait_send())

        @pl.when(self.corner)
        def _():
            for t in range(1, 4):
                self.win_col(t).wait_send()

        @pl.when(self.r == 0)
        def _():
            for t in range(1, 4):
                self.win_row(t, t).wait_send()


SEMAPHORES = ((3,), (8,), (8,), (4,), (4,), (4,), (4,), (4, 4), (4, 4), (4, 4), (4, 4),
              (9,), (8,), (4,), (1,), (4,), (1,), (8,), (8,), (4,), (4,))


def kernel(
    diag_in, panel, trailing_in, own_l, solved, updated,
    dbuf, relay, rows, win, wsrc, pw, q, diag, window, l, schur, trailing, *sems,
):
    e = Exchange(diag_in, panel, dbuf, relay, rows, win, wsrc, pw, q, sems)
    f = Factor(diag, l, schur)

    def assemble(i):
        e.diag_row_wait(i)
        for c in range(4):
            for s in range(8):
                first = 128 * i + 32 * c + 4 * s
                diag[first : first + 4, 0 : 128 * (i + 1)] = dbuf[i, c, s, :, 0 : 128 * (i + 1)]

    own_trailing = pltpu.make_async_copy(trailing_in, trailing, sems[0].at[2])
    own_trailing.start()
    e.enter()
    e.diag_col_send()
    e.own_panel.wait()
    e.rows_col_send(0)
    e.rows_col_send(1)
    e.diag_col_wait()
    e.diag_depth_send()
    e.win_scatter_send()
    e.rows_depth_send(0, e.c, 0)
    e.rows_depth_send(0, e.c, 1)
    e.diag_depth_wait()
    e.diag_row_send()
    e.win_scatter_wait()
    e.win_col_send()
    e.rows_col_send(2)
    e.rows_col_send(3)
    e.rows_pass(0)
    assemble(0)
    f.block(0)
    e.win_col_wait()
    e.win_row_send()
    e.rows_depth_send(0, e.c, 2)
    e.rows_pass(1)
    for i in range(1, 4):
        assemble(i)
    f.rest(0)
    f.block(1)
    e.win_row_wait()
    e.win_depth_send()
    e.rows_depth_send(0, e.c, 3)
    e.rows_pass(2)
    f.rest(1)
    f.block(2)
    e.win_depth_wait()
    e.win_all_send()
    e.rows_pass(3)
    f.rest(2)
    f.block(3)

    position = (e.r * 4 + e.c) * 8 + e.s
    pair = l[pl.ds(pl.multiple_of((position // 2) * 8, 8), 8), :]
    own_l[...] = jnp.where(position % 2 == 0, pair[0:4], pair[4:8])
    own = []
    for k in range(4):
        f.solve_block(relay[e.c, :, at(k)], k, own)
        solved[:, at(k)] = own[k][0]
    e.win_all_wait()
    for s in range(8):
        for r in range(4):
            for u in range(2):
                first = 32 * s + 8 * r + 4 * u
                window[first : first + 4, :] = win[s, r, u]
    w = []
    for k in range(4):
        f.solve_block(window[:, at(k)], k, w)
    own_trailing.wait()
    size = panel.shape[0]
    x = [[] for _ in range(4)]
    total = [None] * 4
    for k in range(4):
        e.rows_wait(k)
        for j in range(4):
            f.solve_block(rows[j, :, at(k)], k, x[j])
            term = dot(x[j][k][1], w[k][1])
            total[j] = term if k == 0 else total[j] + term
    for j in range(4):
        span = slice(size * j, size * (j + 1))
        updated[span, :] = trailing[span, :] - total[j]
    e.leave()


def body(diag_block, panel_rows, trailing):
    vmem = pl.BlockSpec(memory_space=pltpu.VMEM)
    hbm = pl.BlockSpec(memory_space=pltpu.HBM)
    shapes = (
        (4, 4, 8, 4, 512),
        (4, *panel_rows.shape),
        (4, *panel_rows.shape),
        (8, 4, 2, 4, 512),
        (63, 4, 512),
        (4, 8, 4, 512),
        (8, 4, 512),
        (512, 512),
        (256, 512),
        (512, 512),
        (512, 512),
        trailing.shape,
    )
    return pl.pallas_call(
        kernel,
        out_shape=tuple(jax.ShapeDtypeStruct(a.shape, F32) for a in (diag_block, panel_rows, trailing)),
        in_specs=[hbm] * 3,
        out_specs=(vmem,) * 3,
        scratch_shapes=[pltpu.VMEM(shape, F32) for shape in shapes]
        + [pltpu.SemaphoreType.DMA(n) for n in SEMAPHORES],
        compiler_params=pltpu.CompilerParams(
            collective_id=0, has_side_effects=True, vmem_limit_bytes=VMEM_LIMIT
        ),
        name="panel_step",
    )(diag_block, panel_rows, trailing)


VMEM_LIMIT = 60 * 2**20


def solution(mesh):
    specs = (P(ALL, None), P(ALL, None), P(("row", "depth"), "col"))
    return jax.shard_map(body, mesh=mesh, in_specs=specs, out_specs=specs, check_vma=False)
```

profile of v0, /device:TPU:1, one launch (start us, length us, event | category | flops | bytes accessed | tf_op | source)
XLA Modules:
  0.0 65.7 jit_solution(1857579325577209952)
XLA Ops:
  0.6 60.8 %panel_step.1 = (f32[4,512]{1,0:T(4,128)}, f32[252,512]{1,0:T(8,128)}, f32[1008,256]{1,0:T(8,128)}) custom-call(f32[4,512]{1,0:T(4,128)} %diag_in.1, f32[252,512]{1,0:T(8,128)} %panel.1, f32[1008,256]{1,0:T(8,128)} %trailing_in.1), custom_call_target="tpu_custom_call" | custom-call | tf_op jit(solution)/shard_map/panel_step/pallas_call | solution.py:458
  61.5 0.0 copy-start
  61.5 1.4 %copy.9 = f32[4,512]{1,0:T(4,128)} copy(f32[4,512]{1,0:T(4,128)} %get-tuple-element.6) | data formatting | bytes 16384
  62.8 1.9 %copy.10 = f32[252,512]{1,0:T(8,128)} copy(f32[252,512]{1,0:T(8,128)} %get-tuple-element.7) | data formatting | bytes 1032192
  64.7 0.0 copy-done
  64.7 1.0 %copy.11 = f32[1008,256]{1,0:T(8,128)} copy(f32[1008,256]{1,0:T(8,128)S(1)} %copy-done) | data formatting | bytes 2064384
Async XLA Ops:
  61.5 3.3 %copy-start = (f32[1008,256]{1,0:T(8,128)S(1)}, f32[1008,256]{1,0:T(8,128)}, u32[]{:S(2)}) copy-start(f32[1008,256]{1,0:T(8,128)} %get-tuple-element.8) | copy-start | bytes 3096580
where the time goes:
time: 65.9 us; the launch traced here: 65.7 us
  Pallas kernels  60.8 us (92%)
  local copies, waits for them, and re-layouts  4.21 us (6%)
    pallas_call x1, Pallas kernels, body(): pl.pallas_call(kernel, out_shape=tuple((jax.ShapeDtypeStruct(a.shape, F32...  60.8 us
    unnamed x5, local copies, waits for them, and re-layouts  4.21 us

commit v1 on v0

v1 whole, which is shorter than its diff:
```python
import jax
import jax.numpy as jnp
from jax import lax
from jax.experimental import pallas as pl
from jax.experimental.pallas import tpu as pltpu
from jax.sharding import PartitionSpec as P

ALL = ("row", "col", "depth")
F32 = jnp.float32
NT = (((1,), (1,)), ((), ()))
NN = (((1,), (0,)), ((), ()))
BLOCK = 128
MESH = pl.DeviceIdType.MESH


def at(i):
    return slice(BLOCK * i, BLOCK * (i + 1))


def split(x):
    hi = x.astype(jnp.bfloat16)
    return hi, (x - hi.astype(F32)).astype(jnp.bfloat16)


def dot(a, b, dims=NT):
    def one(x, y):
        return lax.dot_general(x, y, dims, preferred_element_type=F32)

    return one(a[0], b[0]) + (one(a[0], b[1]) + one(a[1], b[0]))


def sub(v, k):
    return jnp.broadcast_to(v[k : k + 1, :], (8, 128))


class Block:
    def __init__(self, rows):
        self.ri = lax.broadcasted_iota(jnp.int32, (8, 128), 0)
        self.li = lax.broadcasted_iota(jnp.int32, (8, 128), 1)
        self.rows = rows
        self.unit = jnp.stack([jnp.where(self.li == self.ri + 8 * v, 1.0, 0.0).astype(F32) for v in range(16)])
        self.upper, self.inverse = [], []

    def advance(self, panels):
        ri, li = self.ri, self.li
        for p in panels:
            rows, unit = self.rows, self.unit
            cols = [jnp.broadcast_to(rows[:, :, 8 * p + j : 8 * p + j + 1], rows.shape) for j in range(8)]
            r = [sub(rows[0], k) for k in range(8)]
            s = [sub(unit[0], k) for k in range(8)]
            for k in range(8):
                inv = lax.rsqrt(sub(cols[k][0], k))
                cols[k] = cols[k] * inv
                r[k] = r[k] * inv
                s[k] = s[k] * inv
                for j in range(k + 1, 8):
                    m = sub(cols[k][0], j)
                    cols[j] = cols[j] - cols[k] * m
                    r[j] = r[j] - m * r[k]
                    s[j] = s[j] - m * s[k]
            u, t = r[0], s[0]
            for k in range(1, 8):
                u = jnp.where(ri == k, r[k], u)
                t = jnp.where(ri == k, s[k], t)
            self.upper.append(jnp.where(li >= ri + 8 * p, u, 0.0))
            self.inverse.append(t)
            if p < 15:
                rows, unit = rows[1:], unit[1:]
                for k in range(8):
                    rows = rows - cols[k][1:] * r[k]
                    unit = unit - cols[k][1:] * s[k]
                self.rows, self.unit = rows, unit


class Factor:
    def __init__(self, a, l):
        self.a, self.l = a, l
        self.lows, self.invs, self.below, self.sums = {}, {}, {}, {}

    def column(self, k, i):
        value = self.a[at(i), at(k)]
        for m in range(k):
            value = value - dot(self.lows[i, m], self.lows[k, m])
        return value

    def block(self, k, tasks=(), between=lambda: None):
        value = self.column(k, k)
        b = Block(value.reshape(16, 8, 128))
        tasks = list(tasks)
        for p in range(16):
            b.advance([p])
            if p == 7:
                between()
            for _ in range(-(-len(tasks) // (16 - p))):
                tasks.pop(0)()
        self.invs[k, k] = split(jnp.concatenate(b.inverse, 0))
        self.l[at(k), at(k)] = jnp.concatenate(b.upper, 0).T
        for j in range(k + 1, 4):
            self.l[at(k), at(j)] = jnp.zeros((BLOCK, BLOCK), F32)

    def prepare(self, k, i):
        def task():
            self.below[i] = split(self.column(k, i))

        return task

    def rest(self, k):
        for i in range(k + 1, 4):
            if i not in self.below:
                self.prepare(k, i)()
            low = dot(self.below.pop(i), self.invs[k, k])
            self.l[at(i), at(k)] = low
            self.lows[i, k] = split(low)

    def inverse_sum(self, k, m):
        def task():
            total = dot(self.lows[k, m], self.invs[m, m], NN)
            for j in range(m + 1, k):
                total = total + dot(self.lows[k, j], self.invs[j, m], NN)
            self.sums[k, m] = split(total)

        return task

    def inverse(self, k, m):
        def task():
            self.invs[k, m] = split(-dot(self.invs[k, k], self.sums.pop((k, m)), NN))

        return task

    def solved(self, x, k):
        total = dot(x[0], self.invs[k, 0])
        for m in range(1, k + 1):
            total = total + dot(x[m], self.invs[k, m])
        return total


def remote(src, dst, send, recv, **device):
    return pltpu.make_async_remote_copy(
        src_ref=src, dst_ref=dst, send_sem=send, recv_sem=recv, device_id=device, device_id_type=MESH
    )


class Exchange:
    def __init__(self, diag, panel, dbuf, relay, rows, win, wsrc, wq, hq, pw, sems):
        self.diag, self.panel, self.dbuf, self.relay, self.rows = diag, panel, dbuf, relay, rows
        self.win, self.wsrc, self.wq, self.hq, self.pw = win, wsrc, wq, hq, pw
        (self.loc, self.ds, self.dr, self.cs, self.cr, self.rs, self.rr, self.zs, self.zr, self.xs, self.xr,
         self.w1s, self.w1r, self.w2s, self.w2r, self.w3s, self.w3r, self.w4s, self.w4r, self.w5s, self.w5r) = sems
        self.r, self.c, self.s = (lax.axis_index(a) for a in ALL)
        self.corner = jnp.logical_and(self.r == 0, self.c == 0)

    def enter(self):
        r, c, s = self.r, self.c, self.s
        self.own_diag = pltpu.make_async_copy(self.diag, self.dbuf.at[r, c, s], self.loc.at[0])
        self.own_panel = pltpu.make_async_copy(self.panel, self.relay.at[c], self.loc.at[1])
        self.own_diag.start()
        self.own_panel.start()
        barrier = pltpu.get_barrier_semaphore()
        for axis, me, n in (("depth", s, 8), ("col", c, 4), ("row", r, 4)):
            for t in range(1, n):
                pl.semaphore_signal(barrier, inc=1, device_id={axis: (me + t) % n}, device_id_type=MESH)
        pl.semaphore_wait(barrier, 13)
        self.own_diag.wait()

    def diag_col(self, t, c):
        ref = self.dbuf.at[self.r, c, self.s]
        return remote(ref, ref, self.cs.at[t], self.cr.at[t], col=(self.c + t) % 4)

    def diag_col_send(self):
        for t in range(1, 4):
            self.diag_col(t, self.c).start()

    def diag_col_wait(self):
        for t in range(1, 4):
            self.diag_col(t, (self.c - t) % 4).wait_recv()

    def by_row(self, act):
        for i in range(4):

            @pl.when(self.r == i)
            def _():
                act(i)

    def diag_depth(self, t, s, i, part):
        cols = slice(0, 128) if part == 0 else slice(128, 128 * (i + 1))
        ref = self.dbuf.at[i, :, s, :, cols]
        return remote(ref, ref, self.ds.at[t, part], self.dr.at[t, part], depth=(self.s + t) % 8)

    def diag_depth_each(self, part, act, receive=False):
        def at_row(i):
            if i >= part:
                for t in range(1, 8):
                    act(self.diag_depth(t, (self.s - t) % 8 if receive else self.s, i, part))

        self.by_row(at_row)

    def diag_depth_send(self, part):
        self.diag_depth_each(part, lambda copy: copy.start())

    def diag_depth_wait(self, part):
        self.diag_depth_each(part, lambda copy: copy.wait_recv(), receive=True)

    def diag_row(self, t, i, b):
        ref = self.dbuf.at[i, :, :, :, at(b)]
        return remote(ref, ref, self.rs.at[t, b], self.rr.at[t, b], row=(self.r + t) % 4)

    def diag_row_each(self, b, act):
        def at_row(i):
            if i >= b:
                for t in range(1, 4):
                    act(self.diag_row(t, i, b))

        self.by_row(at_row)

    def diag_row_send(self, b):
        self.diag_row_each(b, lambda copy: copy.start())

    def diag_row_wait(self, src, b):
        def at_row(i):
            if i != src:
                self.diag_row((i - src) % 4, src, b).wait_recv()

        self.by_row(at_row)

    def rows_col(self, t, slot, b):
        ref = self.relay.at[slot, :, at(b)]
        return remote(ref, ref, self.zs.at[t, b], self.zr.at[t, b], col=(self.c + t) % 4)

    def rows_col_send(self, b):
        for t in (1, 3, 2):
            self.rows_col(t, self.c, b).start()

    def rows_pass(self, b):
        for t in (1, 3, 2):
            slot = (self.c - t) % 4
            self.rows_col(t, slot, b).wait_recv()
            self.rows_depth_send(t, slot, b)

    def rows_depth(self, t, slot, b):
        target, j = 2 * slot + self.s // 4, self.s % 4
        return target, remote(
            self.relay.at[slot, :, at(b)], self.rows.at[j, :, at(b)], self.xs.at[t, b], self.xr.at[j, b], depth=target
        )

    def rows_depth_send(self, t, slot, b):
        target, copy = self.rows_depth(t, slot, b)

        @pl.when(target != self.s)
        def _():
            copy.start()

        @pl.when(target == self.s)
        def _():
            self.rows[self.s % 4, :, at(b)] = self.relay[slot, :, at(b)]

    def rows_wait(self, b):
        for j in range(4):
            source = 4 * (self.s % 2) + j
            ref = self.rows.at[j, :, at(b)]

            @pl.when(source != self.s)
            def _():
                remote(ref, ref, self.xs.at[0, b], self.xr.at[j, b], depth=source).wait_recv()

    def corner_case(self, rows, i, act):
        here = jnp.logical_and(self.c == 0, self.s == i)
        if rows is not None:
            here = jnp.logical_and(here, jnp.logical_and(self.r >= rows[0], self.r <= rows[-1]))

        @pl.when(here)
        def _():
            act()

    def win_main(self, i, t):
        n = 16 if t < 3 else 15 - i
        return remote(
            self.wsrc.at[i + 16 * t : i + 16 * t + n], self.wq.at[0:n], self.w1s.at[t], self.w1r.at[0], row=t
        )

    def win_head(self, i):
        return remote(self.wsrc.at[0:i], self.hq.at[0:i], self.w1s.at[4], self.w1r.at[1], row=3)

    def win_scatter(self, act):
        def copies(i):
            if i < 4:
                for t in range(1, 4):
                    act(self.win_main(i, t))
            if i > 0:
                act(self.win_head(i))

        for i in range(5):
            self.corner_case((0,), i, lambda: copies(i))

    def win_scatter_send(self):
        @pl.when(jnp.logical_and(self.corner, self.s < 5))
        def _():
            for u in range(63):
                self.wsrc[u] = self.relay[0, 4 * u : 4 * u + 4, :]

        self.win_scatter(lambda copy: copy.start())

    def win_scatter_wait(self):
        for i in range(5):
            if i < 4:
                self.corner_case((1, 2), i, lambda: self.win_main(i, 1).wait_recv())
                self.corner_case((3,), i, lambda: self.win_main(i, 3).wait_recv())
            if i > 0:
                self.corner_case((3,), i, lambda: self.win_head(i).wait_recv())

    def win_piece(self, rows, i, d):
        n = 2 if rows[0] < 3 else min(max(15 - i - 2 * d, 0), 2)
        if n == 0:
            return None
        src = self.wsrc.at[i + 2 * d : i + 2 * d + n] if rows[0] == 0 else self.wq.at[2 * d : 2 * d + n]
        dst = self.pw.at[i, 0:n]
        return src, dst, lambda: remote(src, dst, self.w2s.at[d], self.w2r.at[i], depth=d)

    def win_head_piece(self, c, d):
        first, last = max(0, 2 * d - 15 + c), min(c + 1, 2 * d - 13 + c)
        if d < 6 or first >= last:
            return None
        slot = (15 - c + first) % 2
        return remote(
            self.hq.at[first:last],
            self.pw.at[c, slot : slot + last - first],
            self.w2s.at[2 + d],
            self.w2r.at[4 + c],
            depth=d,
        )

    def win_spread(self, act, local=False):
        def copies(rows, i):
            for d in range(8):
                if i < 4:
                    piece = self.win_piece(rows, i, d)
                    if piece and d != i:
                        act(piece[2]())
                    elif piece and local:
                        piece[1][...] = piece[0][...]
                if i > 0 and rows[0] == 3:
                    copy = self.win_head_piece(i - 1, d)
                    if copy:
                        act(copy)

        for i in range(5):
            for rows in ((0,), (1, 2), (3,)):
                self.corner_case(rows, i, lambda: copies(rows, i))

    def win_spread_send(self):
        self.win_spread(lambda copy: copy.start(), local=True)

    def win_spread_wait(self):
        def waits(rows, d):
            for i in range(4):
                piece = self.win_piece(rows, i, d)
                if piece and d != i:
                    piece[2]().wait_recv()
                if rows[0] == 3:
                    copy = self.win_head_piece(i, d)
                    if copy:
                        copy.wait_recv()

        for d in range(8):
            for rows in ((0, 1, 2), (3,)):
                self.corner_case(rows, d, lambda: waits(rows, d))

    def win_col(self, t):
        return remote(self.pw.at[t], self.win.at[self.s, self.r], self.w3s.at[t], self.w3r.at[0], col=t)

    def win_col_send(self):
        @pl.when(self.c == 0)
        def _():
            for t in range(1, 4):
                self.win_col(t).start()
            self.win[self.s, self.r] = self.pw[0]

    def win_col_wait(self):
        @pl.when(self.c != 0)
        def _():
            self.win_col(1).wait_recv()

    def win_depth(self, t, d):
        ref = self.win.at[d, self.r]
        return remote(ref, ref, self.w4s.at[t], self.w4r.at[t], depth=(self.s + t) % 8)

    def win_depth_send(self):
        for t in range(1, 8):
            self.win_depth(t, self.s).start()

    def win_depth_wait(self):
        for t in range(1, 8):
            self.win_depth(t, (self.s - t) % 8).wait_recv()

    def win_all(self, t, row):
        ref = self.win.at[:, row]
        return remote(ref, ref, self.w5s.at[t], self.w5r.at[t], row=(self.r + t) % 4)

    def win_all_send(self):
        for t in range(1, 4):
            self.win_all(t, self.r).start()

    def win_all_wait(self):
        for t in range(1, 4):
            self.win_all(t, (self.r - t) % 4).wait_recv()

    def leave(self):
        for t in range(1, 8):
            self.win_depth(t, self.s).wait_send()
        for part in range(2):
            self.diag_depth_each(part, lambda copy: copy.wait_send())
        for b in range(4):
            self.diag_row_each(b, lambda copy: copy.wait_send())
        for t in range(1, 4):
            self.diag_col(t, self.c).wait_send()
            self.win_all(t, self.r).wait_send()
        for b in range(4):
            for t in range(4):
                if t:
                    self.rows_col(t, self.c, b).wait_send()
                target, copy = self.rows_depth(t, (self.c - t) % 4, b)

                @pl.when(target != self.s)
                def _():
                    copy.wait_send()

        self.win_scatter(lambda copy: copy.wait_send())
        self.win_spread(lambda copy: copy.wait_send())

        @pl.when(self.c == 0)
        def _():
            for t in range(1, 4):
                self.win_col(t).wait_send()


SEMAPHORES = ((3,), (8, 2), (8, 2), (4,), (4,), (4, 4), (4, 4), (4, 4), (4, 4), (4, 4), (4, 4),
              (5,), (2,), (10,), (8,), (4,), (1,), (8,), (8,), (4,), (4,))


def kernel(
    diag_in, panel, trailing_in, own_l, solved, updated,
    dbuf, relay, rows, win, wsrc, wq, hq, pw, diag, window, l, trailing, *sems,
):
    e = Exchange(diag_in, panel, dbuf, relay, rows, win, wsrc, wq, hq, pw, sems)
    f = Factor(diag, l)

    def assemble(i, b):
        e.diag_row_wait(i, b)
        for c in range(4):
            for s in range(8):
                first = 128 * i + 32 * c + 4 * s
                diag[first : first + 4, at(b)] = dbuf[i, c, s, :, at(b)]

    def assemble_column(b):
        for i in range(b, 4):
            if i > 0:
                assemble(i, b)

    own_trailing = pltpu.make_async_copy(trailing_in, trailing, sems[0].at[2])
    own_trailing.start()
    e.enter()
    e.diag_col_send()
    e.own_panel.wait()
    e.rows_col_send(0)
    e.win_scatter_send()
    e.rows_col_send(1)
    e.diag_col_wait()
    e.diag_depth_send(0)
    e.diag_depth_send(1)
    e.diag_depth_wait(0)
    e.diag_row_send(0)
    e.diag_depth_wait(1)
    e.diag_row_send(1)
    e.diag_row_send(2)
    e.diag_row_send(3)
    e.win_scatter_wait()
    e.win_spread_send()
    e.rows_depth_send(0, e.c, 0)
    e.rows_depth_send(0, e.c, 1)
    e.rows_pass(0)
    assemble(0, 0)
    e.win_spread_wait()
    e.win_col_send()
    e.rows_col_send(2)

    def first_hook():
        e.rows_col_send(3)

    f.block(0, between=first_hook)
    e.win_col_wait()
    e.win_depth_send()
    e.rows_depth_send(0, e.c, 2)
    e.rows_pass(1)
    assemble_column(0)
    f.rest(0)
    assemble_column(1)

    size = panel.shape[0]
    own_a, rows_a, own_x = {}, [{} for _ in range(4)], {}
    rows_x = [{} for _ in range(4)]

    def own_task(k):
        def task():
            own_a[k] = split(relay[e.c, :, at(k)])
            solved[:, at(k)] = f.solved(own_a, k)

        return task

    def row_task(j, k):
        def task():
            rows_a[j][k] = split(rows[j, :, at(k)])
            rows_x[j][k] = split(f.solved(rows_a[j], k))

        return task

    def second_hook():
        e.rows_depth_send(0, e.c, 3)

    f.block(1, [f.prepare(1, 2), f.prepare(1, 3), own_task(0)], second_hook)
    e.win_depth_wait()
    e.win_all_send()
    e.rows_pass(2)
    f.rest(1)
    assemble_column(2)

    def third_hook():
        e.rows_pass(3)

    f.block(
        2,
        [f.prepare(2, 3), f.inverse_sum(1, 0), f.inverse(1, 0), own_task(1), f.inverse_sum(2, 0), f.inverse_sum(2, 1)],
        third_hook,
    )
    f.rest(2)
    assemble_column(3)
    e.rows_wait(0)
    e.rows_wait(1)
    f.block(
        3,
        [f.inverse(2, 0), f.inverse(2, 1), own_task(2)]
        + [row_task(j, k) for k in range(2) for j in range(4)]
        + [f.inverse_sum(3, m) for m in range(3)],
    )
    for m in range(3):
        f.inverse(3, m)()

    position = (e.r * 4 + e.c) * 8 + e.s
    pair = l[pl.ds(pl.multiple_of((position // 2) * 8, 8), 8), :]
    own_l[...] = jnp.where(position % 2 == 0, pair[0:4], pair[4:8])
    own_task(3)()
    e.win_all_wait()
    for s in range(8):
        for r in range(4):
            for u in range(2):
                first = 64 * r + 8 * s + 4 * u
                window[first : first + 4, :] = win[s, r, u]
    window_a = [split(window[:, at(k)]) for k in range(4)]
    w = [split(f.solved(window_a, k)) for k in range(4)]
    e.rows_wait(2)
    e.rows_wait(3)
    own_trailing.wait()
    for j in range(4):
        row_task(j, 2)()
        row_task(j, 3)()
        total = dot(rows_x[j][0], w[0])
        for k in range(1, 4):
            total = total + dot(rows_x[j][k], w[k])
        span = slice(size * j, size * (j + 1))
        updated[span, :] = trailing[span, :] - total
    e.leave()


def deliver(own_l, solved, updated, own_l_out, solved_out, updated_out, sem):
    copies = [
        pltpu.make_async_copy(src, dst, sem.at[i])
        for i, (src, dst) in enumerate(((own_l, own_l_out), (solved, solved_out), (updated, updated_out)))
    ]
    for copy in copies:
        copy.start()
    for copy in copies:
        copy.wait()


def body(diag_block, panel_rows, trailing):
    vmem = pl.BlockSpec(memory_space=pltpu.VMEM)
    hbm = pl.BlockSpec(memory_space=pltpu.HBM)
    shapes = (
        (4, 4, 8, 4, 512),
        (4, *panel_rows.shape),
        (4, *panel_rows.shape),
        (8, 4, 2, 4, 512),
        (63, 4, 512),
        (16, 4, 512),
        (4, 4, 512),
        (4, 2, 4, 512),
        (512, 512),
        (256, 512),
        (512, 512),
        trailing.shape,
    )
    outs = tuple(jax.ShapeDtypeStruct(a.shape, F32) for a in (diag_block, panel_rows, trailing))
    results = pl.pallas_call(
        kernel,
        out_shape=outs,
        in_specs=[hbm] * 3,
        out_specs=(vmem,) * 3,
        scratch_shapes=[pltpu.VMEM(shape, F32) for shape in shapes]
        + [pltpu.SemaphoreType.DMA(n) for n in SEMAPHORES],
        compiler_params=pltpu.CompilerParams(
            collective_id=0, has_side_effects=True, vmem_limit_bytes=VMEM_LIMIT
        ),
        name="panel_step",
    )(*(pltpu.with_memory_space_constraint(x, pltpu.HBM) for x in (diag_block, panel_rows, trailing)))
    return pl.pallas_call(
        deliver,
        out_shape=outs,
        in_specs=[vmem] * 3,
        out_specs=(hbm,) * 3,
        scratch_shapes=[pltpu.SemaphoreType.DMA((3,))],
        compiler_params=pltpu.CompilerParams(vmem_limit_bytes=2 * 2**20),
        name="deliver",
    )(*results)


VMEM_LIMIT = 44 * 2**20


def solution(mesh):
    specs = (P(ALL, None), P(ALL, None), P(("row", "depth"), "col"))
    return jax.shard_map(body, mesh=mesh, in_specs=specs, out_specs=specs, check_vma=False)
```

time: 65.9 us -> 52.1 us (0.79)
  the two profiles are of different devices: /device:TPU:1 before, /device:TPU:28 now
where the time goes in v1:
time: 52.1 us; the launch traced here: 52 us
  Pallas kernels  51.2 us (98%)
  between operations  0.8 us (2%)
    pallas_call x1, Pallas kernels, body(): pl.pallas_call(kernel, out_shape=outs, in_specs=[hbm] * 3, out_specs=(vme...  50.1 us
    pallas_call x1, Pallas kernels, body(): pl.pallas_call(deliver, out_shape=outs, in_specs=[vmem] * 3, out_specs=(h...  1.17 us

profile of v1, /device:TPU:28, one launch (start us, length us, event | category | flops | bytes accessed | tf_op | source)
XLA Modules:
  0.0 52.0 jit_solution(9266034614928847296)
XLA Ops:
  0.6 50.1 %panel_step.1 = (f32[4,512]{1,0:T(4,128)S(1)}, f32[252,512]{1,0:T(8,128)S(1)}, f32[1008,256]{1,0:T(8,128)S(1)}) custom-call(f32[4,512]{1,0:T(4,128)} %diag_in.1, f32[252,512]{1,0:T(8,128)} %panel.1, f32[1008,256]{1,0:T(8,128)} %trailing_in.1), custom_call_target="tpu_custom_call" | custom-call | tf_op jit(solution)/shard_map/panel_step/pallas_call | solution.py:601
  50.7 1.2 %deliver.1 = (f32[4,512]{1,0:T(4,128)}, f32[252,512]{1,0:T(8,128)}, f32[1008,256]{1,0:T(8,128)}) custom-call(f32[4,512]{1,0:T(4,128)S(1)} %get-tuple-element.6.own_l, f32[252,512]{1,0:T(8,128)S(1)} %get-tuple-element.7.solved, f32[1008,256]{1,0:T(8,128)S(1)} %get-tuple-element.8.updated), custom_call_target="tpu_custom_call" | custom-call | tf_op jit(solution)/shard_map/deliver/pallas_call | solution.py:613

commit v2 on v1

--- a/solution.py
+++ b/solution.py
@@ -17,16 +17,23 @@
     return slice(BLOCK * i, BLOCK * (i + 1))
 
 
+def half(h):
+    return slice(256 * h, 256 * (h + 1))
+
+
 def split(x):
     hi = x.astype(jnp.bfloat16)
     return hi, (x - hi.astype(F32)).astype(jnp.bfloat16)
 
 
 def dot(a, b, dims=NT):
-    def one(x, y):
-        return lax.dot_general(x, y, dims, preferred_element_type=F32)
-
-    return one(a[0], b[0]) + (one(a[0], b[1]) + one(a[1], b[0]))
+    left = jnp.concatenate([a[0], a[1], a[0]], 1)
+    right = jnp.concatenate([b[0], b[0], b[1]], dims[0][1][0])
+    return lax.dot_general(left, right, dims, preferred_element_type=F32)
+
+
+def beside(parts, axis=1):
+    return tuple(jnp.concatenate(x, axis) if len(x) > 1 else x[0] for x in zip(*parts))
 
 
 def sub(v, k):
@@ -38,62 +45,67 @@
         self.ri = lax.broadcasted_iota(jnp.int32, (8, 128), 0)
         self.li = lax.broadcasted_iota(jnp.int32, (8, 128), 1)
         self.rows = rows
-        self.unit = jnp.stack([jnp.where(self.li == self.ri + 8 * v, 1.0, 0.0).astype(F32) for v in range(16)])
         self.upper, self.inverse = [], []
 
-    def advance(self, panels):
-        ri, li = self.ri, self.li
-        for p in panels:
-            rows, unit = self.rows, self.unit
-            cols = [jnp.broadcast_to(rows[:, :, 8 * p + j : 8 * p + j + 1], rows.shape) for j in range(8)]
-            r = [sub(rows[0], k) for k in range(8)]
-            s = [sub(unit[0], k) for k in range(8)]
+    def advance(self, p):
+        ri, li, rows = self.ri, self.li, self.rows
+        first = 8 * p
+        cols = [jnp.broadcast_to(rows[:, :, first + j : first + j + 1], rows.shape) for j in range(8)]
+        e = {(i, j): sub(cols[j][0], i) for j in range(8) for i in range(j, 8)}
+        r = [sub(rows[0], k) for k in range(8)]
+        s = [jnp.where(li < first, r[k], jnp.where(li == first + k, 1.0, 0.0)) for k in range(8)]
+        for k in range(8):
+            inv = lax.rsqrt(e[k, k])
+            m = {j: e[j, k] * inv for j in range(k + 1, 8)}
+            for j in range(k + 1, 8):
+                for i in range(j, 8):
+                    e[i, j] = e[i, j] - m[i] * m[j]
+            cols[k] = cols[k] * inv
+            r[k] = r[k] * inv
+            s[k] = s[k] * inv
+            for j in range(k + 1, 8):
+                cols[j] = cols[j] - cols[k] * m[j]
+                r[j] = r[j] - m[j] * r[k]
+                s[j] = s[j] - m[j] * s[k]
+        u, t = r[0], s[0]
+        for k in range(1, 8):
+            u = jnp.where(ri == k, r[k], u)
+            t = jnp.where(ri == k, s[k], t)
+        self.upper.append(jnp.where(li >= ri + first, u, 0.0))
+        self.inverse.append(t)
+        if p < 15:
+            rows = jnp.where(((li < first) | (li >= first + 8))[None], rows[1:], 0.0)
             for k in range(8):
-                inv = lax.rsqrt(sub(cols[k][0], k))
-                cols[k] = cols[k] * inv
-                r[k] = r[k] * inv
-                s[k] = s[k] * inv
-                for j in range(k + 1, 8):
-                    m = sub(cols[k][0], j)
-                    cols[j] = cols[j] - cols[k] * m
-                    r[j] = r[j] - m * r[k]
-                    s[j] = s[j] - m * s[k]
-            u, t = r[0], s[0]
-            for k in range(1, 8):
-                u = jnp.where(ri == k, r[k], u)
-                t = jnp.where(ri == k, s[k], t)
-            self.upper.append(jnp.where(li >= ri + 8 * p, u, 0.0))
-            self.inverse.append(t)
-            if p < 15:
-                rows, unit = rows[1:], unit[1:]
-                for k in range(8):
-                    rows = rows - cols[k][1:] * r[k]
-                    unit = unit - cols[k][1:] * s[k]
-                self.rows, self.unit = rows, unit
+                rows = rows - cols[k][1:] * jnp.where(li < first + 8, s[k], r[k])
+            self.rows = rows
 
 
 class Factor:
     def __init__(self, a, l):
         self.a, self.l = a, l
-        self.lows, self.invs, self.below, self.sums = {}, {}, {}, {}
+        self.lows, self.inv, self.inv_rows, self.below, self.sums = {}, {}, {}, {}, {}
+
+    def low_row(self, i, n):
+        return beside([self.lows[i, m] for m in range(n)])
 
     def column(self, k, i):
         value = self.a[at(i), at(k)]
-        for m in range(k):
-            value = value - dot(self.lows[i, m], self.lows[k, m])
-        return value
-
-    def block(self, k, tasks=(), between=lambda: None):
+        return value - dot(self.low_row(i, k), self.low_row(k, k)) if k else value
+
+    def block(self, k, tasks=(), between=lambda: None, late=()):
         value = self.column(k, k)
         b = Block(value.reshape(16, 8, 128))
-        tasks = list(tasks)
+        tasks = [list(tasks), list(late)]
         for p in range(16):
-            b.advance([p])
+            b.advance(p)
+            half = tasks[p // 8 if late else 0]
+            for _ in range(-(-len(half) // ((8 if late and p < 8 else 16) - p))):
+                half.pop(0)()
             if p == 7:
                 between()
-            for _ in range(-(-len(tasks) // (16 - p))):
-                tasks.pop(0)()
-        self.invs[k, k] = split(jnp.concatenate(b.inverse, 0))
+        self.inv[k] = split(jnp.concatenate(b.inverse, 0))
+        if k == 0:
+            self.inv_rows[0] = self.inv[0]
         self.l[at(k), at(k)] = jnp.concatenate(b.upper, 0).T
         for j in range(k + 1, 4):
             self.l[at(k), at(j)] = jnp.zeros((BLOCK, BLOCK), F32)
@@ -108,30 +120,33 @@
         for i in range(k + 1, 4):
             if i not in self.below:
                 self.prepare(k, i)()
-            low = dot(self.below.pop(i), self.invs[k, k])
+            low = dot(self.below.pop(i), self.inv[k])
             self.l[at(i), at(k)] = low
             self.lows[i, k] = split(low)
 
-    def inverse_sum(self, k, m):
+    def inverse_rows(self, rows, width):
+        parts = []
+        for k in rows:
+            fill = jnp.zeros((BLOCK, width - BLOCK * (k + 1)), jnp.bfloat16)
+            parts.append(beside([self.inv_rows[k], (fill, fill)]) if fill.shape[1] else self.inv_rows[k])
+        return beside(parts, 0)
+
+    def inverse_sum(self, k):
         def task():
-            total = dot(self.lows[k, m], self.invs[m, m], NN)
-            for j in range(m + 1, k):
-                total = total + dot(self.lows[k, j], self.invs[j, m], NN)
-            self.sums[k, m] = split(total)
+            total = dot(self.low_row(k, k), self.inverse_rows(range(k), BLOCK * k), NN)
+            self.sums[k] = split(total)
 
         return task
 
-    def inverse(self, k, m):
+    def inverse_row(self, k):
         def task():
-            self.invs[k, m] = split(-dot(self.invs[k, k], self.sums.pop((k, m)), NN))
+            left = split(-dot(self.inv[k], self.sums.pop(k), NN))
+            self.inv_rows[k] = beside([left, self.inv[k]])
 
         return task
 
-    def solved(self, x, k):
-        total = dot(x[0], self.invs[k, 0])
-        for m in range(1, k + 1):
-            total = total + dot(x[m], self.invs[k, m])
-        return total
+    def solved(self, x, h):
+        return dot(beside(x[: h + 1]), self.inverse_rows((2 * h, 2 * h + 1), 256 * (h + 1)))
 
 
 def remote(src, dst, send, recv, **device):
@@ -141,24 +156,29 @@
 
 
 class Exchange:
-    def __init__(self, diag, panel, dbuf, relay, rows, win, wsrc, wq, hq, pw, sems):
-        self.diag, self.panel, self.dbuf, self.relay, self.rows = diag, panel, dbuf, relay, rows
+    def __init__(self, diag, panel, own, dbuf, relay, rows, win, wsrc, wq, hq, pw, sems):
+        self.diag, self.panel, self.own, self.dbuf, self.relay, self.rows = diag, panel, own, dbuf, relay, rows
         self.win, self.wsrc, self.wq, self.hq, self.pw = win, wsrc, wq, hq, pw
         (self.loc, self.ds, self.dr, self.cs, self.cr, self.rs, self.rr, self.zs, self.zr, self.xs, self.xr,
-         self.w1s, self.w1r, self.w2s, self.w2r, self.w3s, self.w3r, self.w4s, self.w4r, self.w5s, self.w5r) = sems
+         self.w1s, self.w1r, self.w2s, self.w2r, self.w3s, self.w3r, self.w4s, self.w4r, self.w5s, self.w5r,
+         self.as_, self.ar, self.bs, self.br, self.es, self.er) = sems
         self.r, self.c, self.s = (lax.axis_index(a) for a in ALL)
         self.corner = jnp.logical_and(self.r == 0, self.c == 0)
 
     def enter(self):
         r, c, s = self.r, self.c, self.s
         self.own_diag = pltpu.make_async_copy(self.diag, self.dbuf.at[r, c, s], self.loc.at[0])
-        self.own_panel = pltpu.make_async_copy(self.panel, self.relay.at[c], self.loc.at[1])
+        self.own_panel = pltpu.make_async_copy(self.panel, self.own, self.loc.at[1])
         self.own_diag.start()
         self.own_panel.start()
         barrier = pltpu.get_barrier_semaphore()
         for axis, me, n in (("depth", s, 8), ("col", c, 4), ("row", r, 4)):
             for t in range(1, n):
                 pl.semaphore_signal(barrier, inc=1, device_id={axis: (me + t) % n}, device_id_type=MESH)
+        self.own_panel.wait()
+        n = self.own.shape[0]
+        self.relay[c, 0:n] = self.own[...]
+        self.relay[c, n:256] = jnp.zeros((256 - n, 512), F32)
         pl.semaphore_wait(barrier, 13)
         self.own_diag.wait()
 
@@ -261,6 +281,62 @@
             @pl.when(source != self.s)
             def _():
                 remote(ref, ref, self.xs.at[0, b], self.xr.at[j, b], depth=source).wait_recv()
+
+    def quarter(self, a):
+        return pl.ds(pl.multiple_of(64 * a, 64), 64), slice(256, 512)
+
+    def half_col(self, t, slot, a):
+        ref = self.relay.at[(slot, *self.quarter(a))]
+        return remote(ref, ref, self.as_.at[t], self.ar.at[t], col=(self.c + t) % 4)
+
+    def half_col_send(self):
+        for t in (1, 3, 2):
+            self.half_col(t, self.c, (self.c + t) % 4).start()
+
+    def half_depth(self, t):
+        slot = (self.c - t) % 4
+        target, j, part = 2 * slot + self.s // 4, self.s % 4, self.quarter(self.c)
+        return target, (slot, *part), (j, *part)
+
+    def half_depth_copy(self, t):
+        target, src, dst = self.half_depth(t)
+        return remote(
+            self.relay.at[src], self.rows.at[dst], self.bs.at[t], self.br.at[self.s % 4], depth=target
+        )
+
+    def half_depth_send(self):
+        for t in range(4):
+            if t:
+                self.half_col(t, (self.c - t) % 4, self.c).wait_recv()
+            target, src, dst = self.half_depth(t)
+
+            @pl.when(target != self.s)
+            def _():
+                self.half_depth_copy(t).start()
+
+            @pl.when(target == self.s)
+            def _():
+                self.rows[dst] = self.relay[src]
+
+    def half_all(self, t, a):
+        ref = self.rows.at[(slice(None), *self.quarter(a))]
+        return remote(ref, ref, self.es.at[t], self.er.at[t], col=(self.c + t) % 4)
+
+    def half_all_send(self):
+        for j in range(4):
+            source = 4 * (self.s % 2) + j
+            ref = self.rows.at[(j, *self.quarter(self.c))]
+
+            @pl.when(source != self.s)
+            def _():
+                remote(ref, ref, self.bs.at[0], self.br.at[j], depth=source).wait_recv()
+
+        for t in (1, 3, 2):
+            self.half_all(t, self.c).start()
+
+    def half_all_wait(self):
+        for t in (1, 3, 2):
+            self.half_all(t, (self.c - t) % 4).wait_recv()
 
     def corner_case(self, rows, i, act):
         here = jnp.logical_and(self.c == 0, self.s == i)
@@ -413,7 +489,17 @@
         for t in range(1, 4):
             self.diag_col(t, self.c).wait_send()
             self.win_all(t, self.r).wait_send()
-        for b in range(4):
+        for t in range(4):
+            if t:
+                self.half_col(t, self.c, (self.c + t) % 4).wait_send()
+                self.half_all(t, self.c).wait_send()
+            target = self.half_depth(t)[0]
+
+            @pl.when(target != self.s)
+            def _():
+                self.half_depth_copy(t).wait_send()
+
+        for b in range(2):
             for t in range(4):
                 if t:
                     self.rows_col(t, self.c, b).wait_send()
@@ -432,15 +518,16 @@
                 self.win_col(t).wait_send()
 
 
-SEMAPHORES = ((3,), (8, 2), (8, 2), (4,), (4,), (4, 4), (4, 4), (4, 4), (4, 4), (4, 4), (4, 4),
-              (5,), (2,), (10,), (8,), (4,), (1,), (8,), (8,), (4,), (4,))
+SEMAPHORES = ((3,), (8, 2), (8, 2), (4,), (4,), (4, 4), (4, 4), (4, 2), (4, 2), (4, 2), (4, 2),
+              (5,), (2,), (10,), (8,), (4,), (1,), (8,), (8,), (4,), (4,),
+              (4,), (4,), (4,), (4,), (4,), (4,))
 
 
 def kernel(
     diag_in, panel, trailing_in, own_l, solved, updated,
-    dbuf, relay, rows, win, wsrc, wq, hq, pw, diag, window, l, trailing, *sems,
+    own, dbuf, relay, rows, win, wsrc, wq, hq, pw, diag, window, l, trailing, *sems,
 ):
-    e = Exchange(diag_in, panel, dbuf, relay, rows, win, wsrc, wq, hq, pw, sems)
+    e = Exchange(diag_in, panel, own, dbuf, relay, rows, win, wsrc, wq, hq, pw, sems)
     f = Factor(diag, l)
 
     def assemble(i, b):
@@ -459,113 +546,112 @@
     own_trailing.start()
     e.enter()
     e.diag_col_send()
-    e.own_panel.wait()
+    e.half_col_send()
     e.rows_col_send(0)
     e.win_scatter_send()
     e.rows_col_send(1)
     e.diag_col_wait()
     e.diag_depth_send(0)
     e.diag_depth_send(1)
+    e.half_depth_send()
     e.diag_depth_wait(0)
     e.diag_row_send(0)
+    e.win_scatter_wait()
+    e.win_spread_send()
     e.diag_depth_wait(1)
     e.diag_row_send(1)
     e.diag_row_send(2)
     e.diag_row_send(3)
-    e.win_scatter_wait()
-    e.win_spread_send()
     e.rows_depth_send(0, e.c, 0)
-    e.rows_depth_send(0, e.c, 1)
     e.rows_pass(0)
     assemble(0, 0)
     e.win_spread_wait()
     e.win_col_send()
-    e.rows_col_send(2)
 
     def first_hook():
-        e.rows_col_send(3)
+        e.half_all_send()
 
     f.block(0, between=first_hook)
     e.win_col_wait()
     e.win_depth_send()
-    e.rows_depth_send(0, e.c, 2)
+    e.rows_depth_send(0, e.c, 1)
     e.rows_pass(1)
     assemble_column(0)
     f.rest(0)
     assemble_column(1)
 
     size = panel.shape[0]
-    own_a, rows_a, own_x = {}, [{} for _ in range(4)], {}
-    rows_x = [{} for _ in range(4)]
-
-    def own_task(k):
+    own_a, window_a, w, total = [], [], [], [None] * 4
+    rows_a, rows_x = [[] for _ in range(4)], [[] for _ in range(4)]
+
+    def own_task(h):
         def task():
-            own_a[k] = split(relay[e.c, :, at(k)])
-            solved[:, at(k)] = f.solved(own_a, k)
+            own_a.append(split(own[:, half(h)]))
+            solved[:, half(h)] = f.solved(own_a, h)
 
         return task
 
-    def row_task(j, k):
+    def row_load(j, h):
+        return lambda: rows_a[j].append(split(rows[j, 0:size, half(h)]))
+
+    def row_task(j, h):
+        return lambda: rows_x[j].append(split(f.solved(rows_a[j], h)))
+
+    def window_load():
+        for s in range(8):
+            for r in range(4):
+                for u in range(2):
+                    first = 64 * r + 8 * s + 4 * u
+                    window[first : first + 4, :] = win[s, r, u]
+        for h in range(2):
+            window_a.append(split(window[:, half(h)]))
+
+    def window_task(h):
+        return lambda: w.append(split(f.solved(window_a, h)))
+
+    def product_task(j, h):
         def task():
-            rows_a[j][k] = split(rows[j, :, at(k)])
-            rows_x[j][k] = split(f.solved(rows_a[j], k))
+            term = dot(rows_x[j][h], w[h])
+            total[j] = term if total[j] is None else total[j] + term
 
         return task
 
-    def second_hook():
-        e.rows_depth_send(0, e.c, 3)
-
-    f.block(1, [f.prepare(1, 2), f.prepare(1, 3), own_task(0)], second_hook)
+    f.block(1, [f.prepare(1, 2), f.prepare(1, 3)])
     e.win_depth_wait()
     e.win_all_send()
-    e.rows_pass(2)
     f.rest(1)
     assemble_column(2)
-
-    def third_hook():
-        e.rows_pass(3)
-
-    f.block(
-        2,
-        [f.prepare(2, 3), f.inverse_sum(1, 0), f.inverse(1, 0), own_task(1), f.inverse_sum(2, 0), f.inverse_sum(2, 1)],
-        third_hook,
-    )
+    f.block(2, [f.prepare(2, 3), f.inverse_sum(1), f.inverse_row(1), f.inverse_sum(2), own_task(0)])
     f.rest(2)
     assemble_column(3)
-    e.rows_wait(0)
-    e.rows_wait(1)
+
+    def last_hook():
+        e.rows_wait(0)
+        e.rows_wait(1)
+        e.half_all_wait()
+        e.win_all_wait()
+
     f.block(
         3,
-        [f.inverse(2, 0), f.inverse(2, 1), own_task(2)]
-        + [row_task(j, k) for k in range(2) for j in range(4)]
-        + [f.inverse_sum(3, m) for m in range(3)],
+        [f.inverse_row(2), f.inverse_sum(3)],
+        last_hook,
+        [window_load, window_task(0)]
+        + [t(j, 0) for j in range(4) for t in (row_load, row_task)]
+        + [product_task(j, 0) for j in range(4)]
+        + [row_load(j, 1) for j in range(4)],
     )
-    for m in range(3):
-        f.inverse(3, m)()
-
+    f.inverse_row(3)()
+    window_task(1)()
+    own_trailing.wait()
+    for j in range(4):
+        row_task(j, 1)()
+        product_task(j, 1)()
+        span = slice(size * j, size * (j + 1))
+        updated[span, :] = trailing[span, :] - total[j]
+    own_task(1)()
     position = (e.r * 4 + e.c) * 8 + e.s
     pair = l[pl.ds(pl.multiple_of((position // 2) * 8, 8), 8), :]
     own_l[...] = jnp.where(position % 2 == 0, pair[0:4], pair[4:8])
-    own_task(3)()
-    e.win_all_wait()
-    for s in range(8):
-        for r in range(4):
-            for u in range(2):
-                first = 64 * r + 8 * s + 4 * u
-                window[first : first + 4, :] = win[s, r, u]
-    window_a = [split(window[:, at(k)]) for k in range(4)]
-    w = [split(f.solved(window_a, k)) for k in range(4)]
-    e.rows_wait(2)
-    e.rows_wait(3)
-    own_trailing.wait()
-    for j in range(4):
-        row_task(j, 2)()
-        row_task(j, 3)()
-        total = dot(rows_x[j][0], w[0])
-        for k in range(1, 4):
-            total = total + dot(rows_x[j][k], w[k])
-        span = slice(size * j, size * (j + 1))
-        updated[span, :] = trailing[span, :] - total
     e.leave()
 
 
@@ -584,9 +670,10 @@
     vmem = pl.BlockSpec(memory_space=pltpu.VMEM)
     hbm = pl.BlockSpec(memory_space=pltpu.HBM)
     shapes = (
+        panel_rows.shape,
         (4, 4, 8, 4, 512),
-        (4, *panel_rows.shape),
-        (4, *panel_rows.shape),
+        (4, 256, 512),
+        (4, 256, 512),
         (8, 4, 2, 4, 512),
         (63, 4, 512),
         (16, 4, 512),

time: 52.1 us -> 48 us (0.921)
  the two profiles are of different devices: /device:TPU:28 before, /device:TPU:1 now
where the time goes in v2:
time: 48 us; the launch traced here: 47.9 us
  Pallas kernels  47.1 us (98%)
  between operations  0.8 us (2%)
    pallas_call x1, Pallas kernels, body(): pl.pallas_call(kernel, out_shape=outs, in_specs=[hbm] * 3, out_specs=(vme...  45.9 us
    pallas_call x1, Pallas kernels, body(): pl.pallas_call(deliver, out_shape=outs, in_specs=[vmem] * 3, out_specs=(h...  1.17 us

profile of v2, /device:TPU:1, one launch (start us, length us, event | category | flops | bytes accessed | tf_op | source)
XLA Modules:
  0.0 47.9 jit_solution(10875582429124677926)
XLA Ops:
  0.6 45.9 %panel_step.1 = (f32[4,512]{1,0:T(4,128)S(1)}, f32[252,512]{1,0:T(8,128)S(1)}, f32[1008,256]{1,0:T(8,128)S(1)}) custom-call(f32[4,512]{1,0:T(4,128)} %diag_in.1, f32[252,512]{1,0:T(8,128)} %panel.1, f32[1008,256]{1,0:T(8,128)} %trailing_in.1), custom_call_target="tpu_custom_call" | custom-call | tf_op jit(solution)/shard_map/panel_step/pallas_call | solution.py:688
  46.6 1.2 %deliver.1 = (f32[4,512]{1,0:T(4,128)}, f32[252,512]{1,0:T(8,128)}, f32[1008,256]{1,0:T(8,128)}) custom-call(f32[4,512]{1,0:T(4,128)S(1)} %get-tuple-element.6.own_l, f32[252,512]{1,0:T(8,128)S(1)} %get-tuple-element.7.solved, f32[1008,256]{1,0:T(8,128)S(1)} %get-tuple-element.8.updated), custom_call_target="tpu_custom_call" | custom-call | tf_op jit(solution)/shard_map/deliver/pallas_call | solution.py:700

commit v3 on v2

--- a/solution.py
+++ b/solution.py
@@ -10,6 +10,7 @@
 NT = (((1,), (1,)), ((), ()))
 NN = (((1,), (0,)), ((), ()))
 BLOCK = 128
+NEAR = 4
 MESH = pl.DeviceIdType.MESH
 
 
@@ -17,8 +18,7 @@
     return slice(BLOCK * i, BLOCK * (i + 1))
 
 
-def half(h):
-    return slice(256 * h, 256 * (h + 1))
+PIECES = (((0, 1), slice(0, 256)), ((2,), slice(256, 384)), ((3,), slice(384, 512)))
 
 
 def split(x):
@@ -50,8 +50,11 @@
     def advance(self, p):
         ri, li, rows = self.ri, self.li, self.rows
         first = 8 * p
-        cols = [jnp.broadcast_to(rows[:, :, first + j : first + j + 1], rows.shape) for j in range(8)]
-        e = {(i, j): sub(cols[j][0], i) for j in range(8) for i in range(j, 8)}
+        raw = [jnp.broadcast_to(rows[:, :, first + j : first + j + 1], rows.shape) for j in range(8)]
+        e = {(i, j): sub(raw[j][0], i) for j in range(8) for i in range(j, 8)}
+        near = min(NEAR + 1, rows.shape[0])
+        cols = [x[1:near] for x in raw]
+        scales, factors = [], []
         r = [sub(rows[0], k) for k in range(8)]
         s = [jnp.where(li < first, r[k], jnp.where(li == first + k, 1.0, 0.0)) for k in range(8)]
         for k in range(8):
@@ -60,11 +63,15 @@
             for j in range(k + 1, 8):
                 for i in range(j, 8):
                     e[i, j] = e[i, j] - m[i] * m[j]
-            cols[k] = cols[k] * inv
+            scales.append(inv)
+            factors.append(m)
+            if near > 1:
+                cols[k] = cols[k] * inv
             r[k] = r[k] * inv
             s[k] = s[k] * inv
             for j in range(k + 1, 8):
-                cols[j] = cols[j] - cols[k] * m[j]
+                if near > 1:
+                    cols[j] = cols[j] - cols[k] * m[j]
                 r[j] = r[j] - m[j] * r[k]
                 s[j] = s[j] - m[j] * s[k]
         u, t = r[0], s[0]
@@ -75,8 +82,21 @@
         self.inverse.append(t)
         if p < 15:
             rows = jnp.where(((li < first) | (li >= first + 8))[None], rows[1:], 0.0)
+            both = [jnp.where(li < first + 8, s[k], r[k]) for k in range(8)]
+            close, parts = rows[: near - 1], []
             for k in range(8):
-                rows = rows - cols[k][1:] * jnp.where(li < first + 8, s[k], r[k])
+                close = close - cols[k] * both[k]
+            parts.append(close)
+            if rows.shape[0] > near - 1:
+                for k in range(7, -1, -1):
+                    for j in range(k + 1, 8):
+                        both[k] = both[k] - factors[k][j] * both[j]
+                    both[k] = both[k] * scales[k]
+                far = rows[near - 1 :]
+                for k in range(8):
+                    far = far - raw[k][near:] * both[k]
+                parts.append(far)
+            rows = jnp.concatenate(parts, 0) if len(parts) > 1 else close
             self.rows = rows
 
 
@@ -145,8 +165,9 @@
 
         return task
 
-    def solved(self, x, h):
-        return dot(beside(x[: h + 1]), self.inverse_rows((2 * h, 2 * h + 1), 256 * (h + 1)))
+    def solved(self, x, g):
+        blocks = PIECES[g][0]
+        return dot(beside(x[: g + 1]), self.inverse_rows(blocks, BLOCK * (blocks[-1] + 1)))
 
 
 def remote(src, dst, send, recv, **device):
@@ -235,6 +256,14 @@
     def diag_row_send(self, b):
         self.diag_row_each(b, lambda copy: copy.start())
 
+    def diag_first_send(self, rows):
+        for i in rows:
+
+            @pl.when(self.r == i)
+            def _():
+                for t in range(1, 4):
+                    self.diag_row(t, i, 0).start()
+
     def diag_row_wait(self, src, b):
         def at_row(i):
             if i != src:
@@ -246,15 +275,29 @@
         ref = self.relay.at[slot, :, at(b)]
         return remote(ref, ref, self.zs.at[t, b], self.zr.at[t, b], col=(self.c + t) % 4)
 
+    def rows_far_half(self, t, slot, b):
+        ref = self.relay.at[slot, at((t - 1) // 2), at(b)]
+        return remote(ref, ref, self.zs.at[t - 1, b], self.zr.at[t - 1, b], col=(self.c + t) % 4)
+
     def rows_col_send(self, b):
-        for t in (1, 3, 2):
+        for t in (1, 3):
             self.rows_col(t, self.c, b).start()
 
-    def rows_pass(self, b):
-        for t in (1, 3, 2):
+    def rows_near(self, b):
+        for t in (1, 3):
             slot = (self.c - t) % 4
             self.rows_col(t, slot, b).wait_recv()
-            self.rows_depth_send(t, slot, b)
+            self.rows_far_half(t, slot, b).start()
+
+    def rows_near_pass(self, b):
+        for t in (1, 3):
+            self.rows_depth_send(t, (self.c - t) % 4, b)
+
+    def rows_far_pass(self, b):
+        slot = (self.c + 2) % 4
+        for t in (1, 3):
+            self.rows_far_half(t, slot, b).wait_recv()
+        self.rows_depth_send(2, slot, b)
 
     def rows_depth(self, t, slot, b):
         target, j = 2 * slot + self.s // 4, self.s % 4
@@ -331,12 +374,22 @@
             def _():
                 remote(ref, ref, self.bs.at[0], self.br.at[j], depth=source).wait_recv()
 
-        for t in (1, 3, 2):
+        for t in (1, 3):
             self.half_all(t, self.c).start()
 
-    def half_all_wait(self):
-        for t in (1, 3, 2):
-            self.half_all(t, (self.c - t) % 4).wait_recv()
+    def half_far_half(self, t, a):
+        ref = self.rows.at[(slice(t - 1, t + 1), *self.quarter(a))]
+        return remote(ref, ref, self.es.at[t - 1], self.er.at[t - 1], col=(self.c + t) % 4)
+
+    def half_all_near(self):
+        for t in (1, 3):
+            a = (self.c - t) % 4
+            self.half_all(t, a).wait_recv()
+            self.half_far_half(t, a).start()
+
+    def half_all_far(self):
+        for t in (1, 3):
+            self.half_far_half(t, (self.c + 2) % 4).wait_recv()
 
     def corner_case(self, rows, i, act):
         here = jnp.logical_and(self.c == 0, self.s == i)
@@ -492,7 +545,9 @@
         for t in range(4):
             if t:
                 self.half_col(t, self.c, (self.c + t) % 4).wait_send()
+            if t % 2:
                 self.half_all(t, self.c).wait_send()
+                self.half_far_half(t, (self.c - t) % 4).wait_send()
             target = self.half_depth(t)[0]
 
             @pl.when(target != self.s)
@@ -501,8 +556,9 @@
 
         for b in range(2):
             for t in range(4):
-                if t:
+                if t % 2:
                     self.rows_col(t, self.c, b).wait_send()
+                    self.rows_far_half(t, (self.c - t) % 4, b).wait_send()
                 target, copy = self.rows_depth(t, (self.c - t) % 4, b)
 
                 @pl.when(target != self.s)
@@ -555,27 +611,28 @@
     e.diag_depth_send(1)
     e.half_depth_send()
     e.diag_depth_wait(0)
-    e.diag_row_send(0)
+    e.diag_first_send((0,))
     e.win_scatter_wait()
     e.win_spread_send()
     e.diag_depth_wait(1)
+    e.rows_depth_send(0, e.c, 0)
+    e.rows_near(0)
+    e.rows_near_pass(0)
+    e.diag_first_send((1, 2, 3))
     e.diag_row_send(1)
     e.diag_row_send(2)
     e.diag_row_send(3)
-    e.rows_depth_send(0, e.c, 0)
-    e.rows_pass(0)
     assemble(0, 0)
     e.win_spread_wait()
     e.win_col_send()
-
-    def first_hook():
-        e.half_all_send()
-
-    f.block(0, between=first_hook)
+    e.rows_near(1)
+    e.half_all_send()
+    f.block(0)
     e.win_col_wait()
     e.win_depth_send()
+    e.rows_far_pass(0)
     e.rows_depth_send(0, e.c, 1)
-    e.rows_pass(1)
+    e.rows_near_pass(1)
     assemble_column(0)
     f.rest(0)
     assemble_column(1)
@@ -584,18 +641,18 @@
     own_a, window_a, w, total = [], [], [], [None] * 4
     rows_a, rows_x = [[] for _ in range(4)], [[] for _ in range(4)]
 
-    def own_task(h):
+    def own_task(g):
         def task():
-            own_a.append(split(own[:, half(h)]))
-            solved[:, half(h)] = f.solved(own_a, h)
+            own_a.append(split(own[:, PIECES[g][1]]))
+            solved[:, PIECES[g][1]] = f.solved(own_a, g)
 
         return task
 
-    def row_load(j, h):
-        return lambda: rows_a[j].append(split(rows[j, 0:size, half(h)]))
-
-    def row_task(j, h):
-        return lambda: rows_x[j].append(split(f.solved(rows_a[j], h)))
+    def row_load(j, g):
+        return lambda: rows_a[j].append(split(rows[j, 0:size, PIECES[g][1]]))
+
+    def row_task(j, g):
+        return lambda: rows_x[j].append(split(f.solved(rows_a[j], g)))
 
     def window_load():
         for s in range(8):
@@ -603,52 +660,57 @@
                 for u in range(2):
                     first = 64 * r + 8 * s + 4 * u
                     window[first : first + 4, :] = win[s, r, u]
-        for h in range(2):
-            window_a.append(split(window[:, half(h)]))
-
-    def window_task(h):
-        return lambda: w.append(split(f.solved(window_a, h)))
-
-    def product_task(j, h):
+        for _, columns in PIECES:
+            window_a.append(split(window[:, columns]))
+
+    def window_task(g):
+        return lambda: w.append(split(f.solved(window_a, g)))
+
+    def product_task(j, g):
         def task():
-            term = dot(rows_x[j][h], w[h])
+            term = dot(rows_x[j][g], w[g])
             total[j] = term if total[j] is None else total[j] + term
 
         return task
 
-    f.block(1, [f.prepare(1, 2), f.prepare(1, 3)])
+    def second_hook():
+        e.rows_far_pass(1)
+
+    f.block(1, [f.prepare(1, 2), f.prepare(1, 3)], second_hook)
     e.win_depth_wait()
     e.win_all_send()
+    e.half_all_near()
     f.rest(1)
     assemble_column(2)
     f.block(2, [f.prepare(2, 3), f.inverse_sum(1), f.inverse_row(1), f.inverse_sum(2), own_task(0)])
     f.rest(2)
     assemble_column(3)
 
+    e.rows_wait(0)
+    e.rows_wait(1)
+
     def last_hook():
-        e.rows_wait(0)
-        e.rows_wait(1)
-        e.half_all_wait()
+        e.half_all_far()
         e.win_all_wait()
 
     f.block(
         3,
-        [f.inverse_row(2), f.inverse_sum(3)],
+        [f.inverse_row(2), f.inverse_sum(3), own_task(1)] + [t(j, 0) for j in range(4) for t in (row_load, row_task)],
         last_hook,
-        [window_load, window_task(0)]
-        + [t(j, 0) for j in range(4) for t in (row_load, row_task)]
-        + [product_task(j, 0) for j in range(4)]
-        + [row_load(j, 1) for j in range(4)],
+        [window_load, window_task(0), window_task(1)]
+        + [t(j, 1) for j in range(4) for t in (row_load, row_task)]
+        + [product_task(j, g) for g in range(2) for j in range(4)]
+        + [row_load(j, 2) for j in range(4)],
     )
     f.inverse_row(3)()
-    window_task(1)()
+    window_task(2)()
     own_trailing.wait()
     for j in range(4):
-        row_task(j, 1)()
-        product_task(j, 1)()
+        row_task(j, 2)()
+        product_task(j, 2)()
         span = slice(size * j, size * (j + 1))
         updated[span, :] = trailing[span, :] - total[j]
-    own_task(1)()
+    own_task(2)()
     position = (e.r * 4 + e.c) * 8 + e.s
     pair = l[pl.ds(pl.multiple_of((position // 2) * 8, 8), 8), :]
     own_l[...] = jnp.where(position % 2 == 0, pair[0:4], pair[4:8])

time: 48 us -> 46 us (0.958)
  Pallas kernels: 47.1 us -> 45 us
    pallas_call x1, Pallas kernels: 45.9 us -> 43.9 us  [body(): pl.pallas_call(kernel, out_shape=outs, in_specs=[hbm] * 3, out_specs=(vme...]
where the time goes in v3:
time: 46 us; the launch traced here: 45.8 us
  Pallas kernels  45 us (98%)
  between operations  0.8 us (2%)
    pallas_call x1, Pallas kernels, body(): pl.pallas_call(kernel, out_shape=outs, in_specs=[hbm] * 3, out_specs=(vme...  43.9 us
    pallas_call x1, Pallas kernels, body(): pl.pallas_call(deliver, out_shape=outs, in_specs=[vmem] * 3, out_specs=(h...  1.17 us

profile of v3, /device:TPU:1, one launch (start us, length us, event | category | flops | bytes accessed | tf_op | source)
XLA Modules:
  0.0 45.8 jit_solution(541563818670033712)
XLA Ops:
  0.6 43.9 %panel_step.1 = (f32[4,512]{1,0:T(4,128)S(1)}, f32[252,512]{1,0:T(8,128)S(1)}, f32[1008,256]{1,0:T(8,128)S(1)}) custom-call(f32[4,512]{1,0:T(4,128)} %diag_in.1, f32[252,512]{1,0:T(8,128)} %panel.1, f32[1008,256]{1,0:T(8,128)} %trailing_in.1), custom_call_target="tpu_custom_call" | custom-call | tf_op jit(solution)/shard_map/panel_step/pallas_call | solution.py:750
  44.5 1.2 %deliver.1 = (f32[4,512]{1,0:T(4,128)}, f32[252,512]{1,0:T(8,128)}, f32[1008,256]{1,0:T(8,128)}) custom-call(f32[4,512]{1,0:T(4,128)S(1)} %get-tuple-element.6.own_l, f32[252,512]{1,0:T(8,128)S(1)} %get-tuple-element.7.solved, f32[1008,256]{1,0:T(8,128)S(1)} %get-tuple-element.8.updated), custom_call_target="tpu_custom_call" | custom-call | tf_op jit(solution)/shard_map/deliver/pallas_call | solution.py:762

commit v4 on v3

--- a/solution.py
+++ b/solution.py
@@ -11,6 +11,7 @@
 NN = (((1,), (0,)), ((), ()))
 BLOCK = 128
 NEAR = 4
+ROWS_AT, LAST_AT = 4, 8
 MESH = pl.DeviceIdType.MESH
 
 
@@ -112,17 +113,17 @@
         value = self.a[at(i), at(k)]
         return value - dot(self.low_row(i, k), self.low_row(k, k)) if k else value
 
-    def block(self, k, tasks=(), between=lambda: None, late=()):
+    def block(self, k, tasks=(), hooks=()):
         value = self.column(k, k)
         b = Block(value.reshape(16, 8, 128))
-        tasks = [list(tasks), list(late)]
-        for p in range(16):
-            b.advance(p)
-            half = tasks[p // 8 if late else 0]
-            for _ in range(-(-len(half) // ((8 if late and p < 8 else 16) - p))):
-                half.pop(0)()
-            if p == 7:
-                between()
+        stages = [(0, lambda: None, tasks), *hooks, (16, None, ())]
+        for (start, wait, work), (end, _, _) in zip(stages, stages[1:]):
+            wait()
+            work = list(work)
+            for p in range(start, end):
+                b.advance(p)
+                for _ in range(-(-len(work) // (end - p))):
+                    work.pop(0)()
         self.inv[k] = split(jnp.concatenate(b.inverse, 0))
         if k == 0:
             self.inv_rows[0] = self.inv[0]
@@ -181,7 +182,7 @@
         self.diag, self.panel, self.own, self.dbuf, self.relay, self.rows = diag, panel, own, dbuf, relay, rows
         self.win, self.wsrc, self.wq, self.hq, self.pw = win, wsrc, wq, hq, pw
         (self.loc, self.ds, self.dr, self.cs, self.cr, self.rs, self.rr, self.zs, self.zr, self.xs, self.xr,
-         self.w1s, self.w1r, self.w2s, self.w2r, self.w3s, self.w3r, self.w4s, self.w4r, self.w5s, self.w5r,
+         self.w1s, self.w1r, self.w2s, self.w2r, self.w3s, self.w3r, self.w4s, self.w4r, self.w5s, self.w5r, self.w6s, self.w6r,
          self.as_, self.ar, self.bs, self.br, self.es, self.er) = sems
         self.r, self.c, self.s = (lax.axis_index(a) for a in ALL)
         self.corner = jnp.logical_and(self.r == 0, self.c == 0)
@@ -494,34 +495,37 @@
                 self.corner_case(rows, d, lambda: waits(rows, d))
 
     def win_col(self, t):
-        return remote(self.pw.at[t], self.win.at[self.s, self.r], self.w3s.at[t], self.w3r.at[0], col=t)
+        return remote(self.pw.at[t], self.win_at(self.s), self.w3s.at[t], self.w3r.at[0], col=t)
 
     def win_col_send(self):
         @pl.when(self.c == 0)
         def _():
             for t in range(1, 4):
                 self.win_col(t).start()
-            self.win[self.s, self.r] = self.pw[0]
+            self.win[self.s // 2, self.s % 2, self.r] = self.pw[0]
 
     def win_col_wait(self):
         @pl.when(self.c != 0)
         def _():
             self.win_col(1).wait_recv()
 
+    def win_at(self, d):
+        return self.win.at[d // 2, d % 2, self.r]
+
     def win_depth(self, t, d):
-        ref = self.win.at[d, self.r]
+        ref = self.win_at(d)
         return remote(ref, ref, self.w4s.at[t], self.w4r.at[t], depth=(self.s + t) % 8)
 
     def win_depth_send(self):
-        for t in range(1, 8):
+        for t in (2, 4, 6):
             self.win_depth(t, self.s).start()
 
     def win_depth_wait(self):
-        for t in range(1, 8):
+        for t in (2, 4, 6):
             self.win_depth(t, (self.s - t) % 8).wait_recv()
 
     def win_all(self, t, row):
-        ref = self.win.at[:, row]
+        ref = self.win.at[:, self.s % 2, row]
         return remote(ref, ref, self.w5s.at[t], self.w5r.at[t], row=(self.r + t) % 4)
 
     def win_all_send(self):
@@ -532,8 +536,18 @@
         for t in range(1, 4):
             self.win_all(t, (self.r - t) % 4).wait_recv()
 
-    def leave(self):
-        for t in range(1, 8):
+    def win_pair(self, core):
+        ref = self.win.at[:, core]
+        return remote(ref, ref, self.w6s.at[0], self.w6r.at[0], depth=self.s + 1 - 2 * (self.s % 2))
+
+    def win_pair_send(self):
+        self.win_pair(self.s % 2).start()
+
+    def win_pair_wait(self):
+        self.win_pair(1 - self.s % 2).wait_recv()
+
+    def leave_early(self):
+        for t in (2, 4, 6):
             self.win_depth(t, self.s).wait_send()
         for part in range(2):
             self.diag_depth_each(part, lambda copy: copy.wait_send())
@@ -541,13 +555,8 @@
             self.diag_row_each(b, lambda copy: copy.wait_send())
         for t in range(1, 4):
             self.diag_col(t, self.c).wait_send()
-            self.win_all(t, self.r).wait_send()
+            self.half_col(t, self.c, (self.c + t) % 4).wait_send()
         for t in range(4):
-            if t:
-                self.half_col(t, self.c, (self.c + t) % 4).wait_send()
-            if t % 2:
-                self.half_all(t, self.c).wait_send()
-                self.half_far_half(t, (self.c - t) % 4).wait_send()
             target = self.half_depth(t)[0]
 
             @pl.when(target != self.s)
@@ -555,16 +564,9 @@
                 self.half_depth_copy(t).wait_send()
 
         for b in range(2):
-            for t in range(4):
-                if t % 2:
-                    self.rows_col(t, self.c, b).wait_send()
-                    self.rows_far_half(t, (self.c - t) % 4, b).wait_send()
-                target, copy = self.rows_depth(t, (self.c - t) % 4, b)
-
-                @pl.when(target != self.s)
-                def _():
-                    copy.wait_send()
-
+            for t in (1, 3):
+                self.rows_col(t, self.c, b).wait_send()
+                self.rows_far_half(t, (self.c - t) % 4, b).wait_send()
         self.win_scatter(lambda copy: copy.wait_send())
         self.win_spread(lambda copy: copy.wait_send())
 
@@ -573,9 +575,24 @@
             for t in range(1, 4):
                 self.win_col(t).wait_send()
 
+    def leave(self):
+        self.win_pair(self.s % 2).wait_send()
+        for t in range(1, 4):
+            self.win_all(t, self.r).wait_send()
+        for t in (1, 3):
+            self.half_all(t, self.c).wait_send()
+            self.half_far_half(t, (self.c - t) % 4).wait_send()
+        for b in range(2):
+            for t in range(4):
+                target, copy = self.rows_depth(t, (self.c - t) % 4, b)
+
+                @pl.when(target != self.s)
+                def _():
+                    copy.wait_send()
+
 
 SEMAPHORES = ((3,), (8, 2), (8, 2), (4,), (4,), (4, 4), (4, 4), (4, 2), (4, 2), (4, 2), (4, 2),
-              (5,), (2,), (10,), (8,), (4,), (1,), (8,), (8,), (4,), (4,),
+              (5,), (2,), (10,), (8,), (4,), (1,), (8,), (8,), (4,), (4,), (1,), (1,),
               (4,), (4,), (4,), (4,), (4,), (4,))
 
 
@@ -659,7 +676,7 @@
             for r in range(4):
                 for u in range(2):
                     first = 64 * r + 8 * s + 4 * u
-                    window[first : first + 4, :] = win[s, r, u]
+                    window[first : first + 4, :] = win[s // 2, s % 2, r, u]
         for _, columns in PIECES:
             window_a.append(split(window[:, columns]))
 
@@ -676,7 +693,7 @@
     def second_hook():
         e.rows_far_pass(1)
 
-    f.block(1, [f.prepare(1, 2), f.prepare(1, 3)], second_hook)
+    f.block(1, [f.prepare(1, 2), f.prepare(1, 3)], [(8, second_hook, ())])
     e.win_depth_wait()
     e.win_all_send()
     e.half_all_near()
@@ -686,21 +703,33 @@
     f.rest(2)
     assemble_column(3)
 
-    e.rows_wait(0)
-    e.rows_wait(1)
+
+    e.win_all_wait()
+    e.win_pair_send()
+
+    def rows_hook():
+        e.rows_wait(0)
+        e.rows_wait(1)
 
     def last_hook():
+        e.leave_early()
         e.half_all_far()
-        e.win_all_wait()
+        e.win_pair_wait()
 
     f.block(
         3,
-        [f.inverse_row(2), f.inverse_sum(3), own_task(1)] + [t(j, 0) for j in range(4) for t in (row_load, row_task)],
-        last_hook,
-        [window_load, window_task(0), window_task(1)]
-        + [t(j, 1) for j in range(4) for t in (row_load, row_task)]
-        + [product_task(j, g) for g in range(2) for j in range(4)]
-        + [row_load(j, 2) for j in range(4)],
+        [f.inverse_row(2), f.inverse_sum(3), own_task(1)],
+        [
+            (ROWS_AT, rows_hook, [t(j, 0) for j in range(4) for t in (row_load, row_task)]),
+            (
+                LAST_AT,
+                last_hook,
+                [window_load, window_task(0), window_task(1)]
+                + [t(j, 1) for j in range(4) for t in (row_load, row_task)]
+                + [product_task(j, g) for g in range(2) for j in range(4)]
+                + [row_load(j, 2) for j in range(4)],
+            ),
+        ],
     )
     f.inverse_row(3)()
     window_task(2)()
@@ -736,7 +765,7 @@
         (4, 4, 8, 4, 512),
         (4, 256, 512),
         (4, 256, 512),
-        (8, 4, 2, 4, 512),
+        (4, 2, 4, 2, 4, 512),
         (63, 4, 512),
         (16, 4, 512),
         (4, 4, 512),

time: 46 us -> 44.2 us (0.961)
  Pallas kernels: 45 us -> 43.3 us
    pallas_call x1, Pallas kernels: 43.9 us -> 42.1 us  [body(): pl.pallas_call(kernel, out_shape=outs, in_specs=[hbm] * 3, out_specs=(vme...]
where the time goes in v4:
time: 44.2 us; the launch traced here: 44.1 us
  Pallas kernels  43.3 us (98%)
  between operations  0.8 us (2%)
    pallas_call x1, Pallas kernels, body(): pl.pallas_call(kernel, out_shape=outs, in_specs=[hbm] * 3, out_specs=(vme...  42.1 us
    pallas_call x1, Pallas kernels, body(): pl.pallas_call(deliver, out_shape=outs, in_specs=[vmem] * 3, out_specs=(h...  1.17 us

profile of v4, /device:TPU:1, one launch (start us, length us, event | category | flops | bytes accessed | tf_op | source)
XLA Modules:
  0.0 44.1 jit_solution(11016620159759499947)
XLA Ops:
  0.6 42.1 %panel_step.1 = (f32[4,512]{1,0:T(4,128)S(1)}, f32[252,512]{1,0:T(8,128)S(1)}, f32[1008,256]{1,0:T(8,128)S(1)}) custom-call(f32[4,512]{1,0:T(4,128)} %diag_in.1, f32[252,512]{1,0:T(8,128)} %panel.1, f32[1008,256]{1,0:T(8,128)} %trailing_in.1), custom_call_target="tpu_custom_call" | custom-call | tf_op jit(solution)/shard_map/panel_step/pallas_call | solution.py:779
  42.8 1.2 %deliver.1 = (f32[4,512]{1,0:T(4,128)}, f32[252,512]{1,0:T(8,128)}, f32[1008,256]{1,0:T(8,128)}) custom-call(f32[4,512]{1,0:T(4,128)S(1)} %get-tuple-element.6.own_l, f32[252,512]{1,0:T(8,128)S(1)} %get-tuple-element.7.solved, f32[1008,256]{1,0:T(8,128)S(1)} %get-tuple-element.8.updated), custom_call_target="tpu_custom_call" | custom-call | tf_op jit(solution)/shard_map/deliver/pallas_call | solution.py:791

commit v5 on v4

--- a/solution.py
+++ b/solution.py
@@ -11,7 +11,7 @@
 NN = (((1,), (0,)), ((), ()))
 BLOCK = 128
 NEAR = 4
-ROWS_AT, LAST_AT = 4, 8
+ROWS_AT, LAST_AT = 3, 9
 MESH = pl.DeviceIdType.MESH
 
 
@@ -197,12 +197,14 @@
         for axis, me, n in (("depth", s, 8), ("col", c, 4), ("row", r, 4)):
             for t in range(1, n):
                 pl.semaphore_signal(barrier, inc=1, device_id={axis: (me + t) % n}, device_id_type=MESH)
+        pl.semaphore_wait(barrier, 13)
+        self.own_diag.wait()
+
+    def load_panel(self):
         self.own_panel.wait()
         n = self.own.shape[0]
-        self.relay[c, 0:n] = self.own[...]
-        self.relay[c, n:256] = jnp.zeros((256 - n, 512), F32)
-        pl.semaphore_wait(barrier, 13)
-        self.own_diag.wait()
+        self.relay[self.c, 0:n] = self.own[...]
+        self.relay[self.c, n:256] = jnp.zeros((256 - n, 512), F32)
 
     def diag_col(self, t, c):
         ref = self.dbuf.at[self.r, c, self.s]
@@ -616,9 +618,10 @@
                 assemble(i, b)
 
     own_trailing = pltpu.make_async_copy(trailing_in, trailing, sems[0].at[2])
-    own_trailing.start()
     e.enter()
     e.diag_col_send()
+    own_trailing.start()
+    e.load_panel()
     e.half_col_send()
     e.rows_col_send(0)
     e.win_scatter_send()
@@ -704,10 +707,9 @@
     assemble_column(3)
 
 
-    e.win_all_wait()
-    e.win_pair_send()
-
     def rows_hook():
+        e.win_all_wait()
+        e.win_pair_send()
         e.rows_wait(0)
         e.rows_wait(1)
 
@@ -747,10 +749,12 @@
 
 
 def deliver(own_l, solved, updated, own_l_out, solved_out, updated_out, sem):
-    copies = [
-        pltpu.make_async_copy(src, dst, sem.at[i])
-        for i, (src, dst) in enumerate(((own_l, own_l_out), (solved, solved_out), (updated, updated_out)))
-    ]
+    rows = updated.shape[0]
+    parts = [(own_l, own_l_out), (solved, solved_out)]
+    for first in range(0, rows, 256):
+        part = pl.ds(first, min(256, rows - first))
+        parts.append((updated.at[part], updated_out.at[part]))
+    copies = [pltpu.make_async_copy(src, dst, sem.at[i]) for i, (src, dst) in enumerate(parts)]
     for copy in copies:
         copy.start()
     for copy in copies:
@@ -793,7 +797,7 @@
         out_shape=outs,
         in_specs=[vmem] * 3,
         out_specs=(hbm,) * 3,
-        scratch_shapes=[pltpu.SemaphoreType.DMA((3,))],
+        scratch_shapes=[pltpu.SemaphoreType.DMA((6,))],
         compiler_params=pltpu.CompilerParams(vmem_limit_bytes=2 * 2**20),
         name="deliver",
     )(*results)

time: 44.2 us -> 44.2 us (level)
  no operation moved by 1% of the time
where the time goes in v5:
time: 44.2 us; the launch traced here: 44 us
  Pallas kernels  43.2 us (98%)
  between operations  0.8 us (2%)
    pallas_call x1, Pallas kernels, body(): pl.pallas_call(kernel, out_shape=outs, in_specs=[hbm] * 3, out_specs=(vme...  42 us
    pallas_call x1, Pallas kernels, body(): pl.pallas_call(deliver, out_shape=outs, in_specs=[vmem] * 3, out_specs=(h...  1.18 us

profile of v5, /device:TPU:1, one launch (start us, length us, event | category | flops | bytes accessed | tf_op | source)
XLA Modules:
  0.0 44.0 jit_solution(14611364998903305295)
XLA Ops:
  0.6 42.0 %panel_step.1 = (f32[4,512]{1,0:T(4,128)S(1)}, f32[252,512]{1,0:T(8,128)S(1)}, f32[1008,256]{1,0:T(8,128)S(1)}) custom-call(f32[4,512]{1,0:T(4,128)} %diag_in.1, f32[252,512]{1,0:T(8,128)} %panel.1, f32[1008,256]{1,0:T(8,128)} %trailing_in.1), custom_call_target="tpu_custom_call" | custom-call | tf_op jit(solution)/shard_map/panel_step/pallas_call | solution.py:783
  42.7 1.2 %deliver.1 = (f32[4,512]{1,0:T(4,128)}, f32[252,512]{1,0:T(8,128)}, f32[1008,256]{1,0:T(8,128)}) custom-call(f32[4,512]{1,0:T(4,128)S(1)} %get-tuple-element.6.own_l, f32[252,512]{1,0:T(8,128)S(1)} %get-tuple-element.7.solved, f32[1008,256]{1,0:T(8,128)S(1)} %get-tuple-element.8.updated), custom_call_target="tpu_custom_call" | custom-call | tf_op jit(solution)/shard_map/deliver/pallas_call | solution.py:795

commit v6 on v5

--- a/solution.py
+++ b/solution.py
@@ -11,7 +11,7 @@
 NN = (((1,), (0,)), ((), ()))
 BLOCK = 128
 NEAR = 4
-ROWS_AT, LAST_AT = 3, 9
+FIRST_AT, ROWS_AT, LAST_AT = 6, 3, 9
 MESH = pl.DeviceIdType.MESH
 
 
@@ -647,10 +647,13 @@
     e.win_col_send()
     e.rows_near(1)
     e.half_all_send()
-    f.block(0)
+
+    def first_hook():
+        e.rows_far_pass(0)
+
+    f.block(0, hooks=[(FIRST_AT, first_hook, ())])
     e.win_col_wait()
     e.win_depth_send()
-    e.rows_far_pass(0)
     e.rows_depth_send(0, e.c, 1)
     e.rows_near_pass(1)
     assemble_column(0)

time: 44.2 us -> 44.3 us (level)
  no operation moved by 1% of the time
where the time goes in v6:
time: 44.3 us; the launch traced here: 44.1 us
  Pallas kernels  43.4 us (98%)
  between operations  0.8 us (2%)
    pallas_call x1, Pallas kernels, body(): pl.pallas_call(kernel, out_shape=outs, in_specs=[hbm] * 3, out_specs=(vme...  42.2 us
    pallas_call x1, Pallas kernels, body(): pl.pallas_call(deliver, out_shape=outs, in_specs=[vmem] * 3, out_specs=(h...  1.18 us

profile of v6, /device:TPU:1, one launch (start us, length us, event | category | flops | bytes accessed | tf_op | source)
XLA Modules:
  0.0 44.1 jit_solution(2373787970062295366)
XLA Ops:
  0.6 42.2 %panel_step.1 = (f32[4,512]{1,0:T(4,128)S(1)}, f32[252,512]{1,0:T(8,128)S(1)}, f32[1008,256]{1,0:T(8,128)S(1)}) custom-call(f32[4,512]{1,0:T(4,128)} %diag_in.1, f32[252,512]{1,0:T(8,128)} %panel.1, f32[1008,256]{1,0:T(8,128)} %trailing_in.1), custom_call_target="tpu_custom_call" | custom-call | tf_op jit(solution)/shard_map/panel_step/pallas_call | solution.py:786
  42.8 1.2 %deliver.1 = (f32[4,512]{1,0:T(4,128)}, f32[252,512]{1,0:T(8,128)}, f32[1008,256]{1,0:T(8,128)}) custom-call(f32[4,512]{1,0:T(4,128)S(1)} %get-tuple-element.6.own_l, f32[252,512]{1,0:T(8,128)S(1)} %get-tuple-element.7.solved, f32[1008,256]{1,0:T(8,128)S(1)} %get-tuple-element.8.updated), custom_call_target="tpu_custom_call" | custom-call | tf_op jit(solution)/shard_map/deliver/pallas_call | solution.py:798
